TPU v7x, 128 devices: a whole 4x4x4 slice. The times are simulated.
128 devices in a mesh: tok: 16 (over z, x), mp: 8 (over y, core).
Axes of the slice: x: 4, y: 4, z: 4, core: 2. Of those that a mesh axis runs over, the one named last changes fastest.
Arguments:
- tokens: bfloat16 [6144, 2048], P('tok', 'mp'), may hold values from -120 to 120
- norm_gain: float32 [2048], replicated, may hold values from 0.5 to 1.5
- running_sq: float32 [2048], P('mp'), may hold values from 0.5 to 4
- gate_weight: bfloat16 [2048, 8192], P(None, 'mp'), may hold values from -0.125 to 0.125
- up_weight: bfloat16 [2048, 8192], P(None, 'mp'), may hold values from -0.125 to 0.125
- down_weight_t: bfloat16 [2048, 8192], P(None, 'mp'), may hold values from -0.0625 to 0.0625
- groups: int32 [384], P('tok'), may hold values from 0 to 47, as said below
- cotangent: bfloat16 [6144, 2048], P('tok', 'mp'), may hold values from -6 to 6
Outputs:
- block_out: bfloat16 [6144, 2048], P('tok', 'mp')
- grad_tokens: bfloat16 [6144, 2048], P('tok', 'mp')
- running_new: float32 [2048], P('mp')
- grad_gain: float32 [2048], P('mp')
- grad_gate: float32 [2048, 8192], P('tok', 'mp')
- grad_up: float32 [2048, 8192], P('tok', 'mp')
- grad_down_t: float32 [2048, 8192], P('tok', 'mp')
Inputs may be any that keep to these rules, and one draw needn't show every extreme that they name: Each of the 48 ghost groups holds exactly 8 blocks.
All inputs are finite; a program needn't handle non-finite values.
Results may differ from a plain program's by a relative error of at most 0.02.
Values may be sent and summed in bfloat16 or wider, within the bound.
No kernel may reach another device: no remote copies, remote signals or barrier semaphores. Data moves between devices by JAX's collectives and lax.ppermute only.
A program may use at most 128 MiB of HBM per device.

v0:
```python
import jax
import jax.numpy as jnp
from jax import lax
from jax.sharding import PartitionSpec as P

GHOST = 128
BLK = 16


epsilon = 1e-05
momentum = 0.1
highest = lax.Precision.HIGHEST


def from_everyone(x, axis):
    copies = jnp.broadcast_to(x, (lax.axis_size(axis), *x.shape))
    return lax.all_to_all(copies, axis, split_axis=0, concat_axis=0, tiled=True)


def of_everyone(x, axis):
    everything = from_everyone(x, axis)
    return jnp.sum(everything, axis=0)


def laid_out(pieces, dim):
    pieces = jnp.moveaxis(pieces, 0, dim)
    lengths = pieces.shape
    return pieces.reshape(*lengths[:dim], lengths[dim] * lengths[dim + 1], *lengths[dim + 2 :])


def gathered_copies(x, axis, dim):
    return laid_out(from_everyone(x, axis), dim)


def split_up(x, dim, count):
    before, after = (x.shape[:dim], x.shape[dim + 1 :])
    return jnp.moveaxis(x.reshape(*before, count, -1, *after), dim, 0)


def sent_and_summed(x, axis, dim):
    count = lax.axis_size(axis)
    pieces = lax.all_to_all(split_up(x, dim, count), axis, 0, 0, tiled=True)
    return jnp.sum(pieces.astype(jnp.float32), axis=0)


def of_everyone_2(x, axis):
    everything = from_everyone(x, axis)
    return jnp.sum(everything.astype(jnp.float32), axis=0)


def group_sums(values, onehot):
    blocks = values.reshape(values.shape[0] // BLK, BLK, values.shape[1]).sum(axis=1)
    return jnp.dot(onehot, blocks, precision=highest, preferred_element_type=jnp.float32)


def per_token(table, onehot):
    per_block = jnp.dot(onehot.T, table, precision=highest, preferred_element_type=jnp.float32)
    wide = jnp.broadcast_to(per_block[:, None, :], (per_block.shape[0], BLK, per_block.shape[1]))
    return wide.reshape(per_block.shape[0] * BLK, per_block.shape[1])


def contract_rows(left, right):
    return lax.dot_general(
        left, right, (((0,), (0,)), ((), ())), preferred_element_type=jnp.float32
    )


def contract_cols(left, right):
    return lax.dot_general(
        left, right, (((1,), (1,)), ((), ())), preferred_element_type=jnp.float32
    )


def body(tokens, norm_gain, running_sq, gate_weight, up_weight, down_weight_t, groups, cotangent):
    tok_count = lax.axis_size("tok")
    tok_rows, feat_width = tokens.shape
    groups_total = tok_rows * tok_count // GHOST
    onehot = (groups[None, :] == jnp.arange(groups_total, dtype=jnp.int32)[:, None]).astype(
        jnp.float32
    )
    col_first = lax.axis_index("mp") * feat_width
    x_local = tokens.astype(jnp.float32)
    gain_local = lax.dynamic_slice_in_dim(norm_gain, col_first, feat_width, 0)
    quad_mean = of_everyone(group_sums(x_local * x_local, onehot), "tok") / GHOST
    scale = per_token(lax.rsqrt(quad_mean + epsilon), onehot)
    normed = x_local * scale
    hid_in = gathered_copies((gain_local * normed).astype(jnp.bfloat16), "mp", 1)
    dy_full = gathered_copies(cotangent, "mp", 1)
    gate = jnp.dot(hid_in, gate_weight, preferred_element_type=jnp.float32)
    lift = jnp.dot(hid_in, up_weight, preferred_element_type=jnp.float32)
    sigma = jax.nn.sigmoid(gate)
    hidden = (gate * sigma * lift).astype(jnp.bfloat16)
    branch = sent_and_summed(contract_cols(hidden, down_weight_t).astype(jnp.bfloat16), "mp", 1)
    block_out = (x_local + branch).astype(jnp.bfloat16)
    running_new = (1.0 - momentum) * running_sq + momentum * jnp.mean(quad_mean, axis=0)
    grad_hidden = jnp.dot(dy_full, down_weight_t, preferred_element_type=jnp.float32)
    grad_gate_in = (grad_hidden * lift * sigma * (1.0 + gate * (1.0 - sigma))).astype(jnp.bfloat16)
    grad_lift = (grad_hidden * gate * sigma).astype(jnp.bfloat16)
    grad_partial = contract_cols(grad_gate_in, gate_weight) + contract_cols(grad_lift, up_weight)
    grad_normed_in = sent_and_summed(grad_partial.astype(jnp.bfloat16), "mp", 1)
    partial_value = of_everyone_2(
        group_sums(grad_normed_in * normed, onehot).astype(jnp.bfloat16), "tok"
    ).astype(jnp.float32)
    grad_gain = jnp.sum(partial_value, axis=0)
    mean_term = per_token(gain_local * partial_value / GHOST, onehot)
    grad_tokens = (
        cotangent.astype(jnp.float32) + scale * (gain_local * grad_normed_in - normed * mean_term)
    ).astype(jnp.bfloat16)
    both_grads = jnp.concatenate([grad_gate_in, grad_lift], axis=1)
    hidden_width = gate_weight.shape[1]
    upper = contract_rows(hid_in, both_grads)
    lower = contract_rows(dy_full, hidden)
    weight_total = lax.psum_scatter(
        jnp.concatenate([upper, lower], axis=1).astype(jnp.bfloat16),
        "tok",
        scatter_dimension=0,
        tiled=True,
    ).astype(jnp.float32)
    grad_gate = weight_total[:, :hidden_width]
    grad_up = weight_total[:, hidden_width : 2 * hidden_width]
    grad_down_t = weight_total[:, 2 * hidden_width :]
    return (block_out, grad_tokens, running_new, grad_gain, grad_gate, grad_up, grad_down_t)


def solution(mesh):
    placed = (
        P("tok", "mp"),
        P(),
        P("mp"),
        P(None, "mp"),
        P(None, "mp"),
        P(None, "mp"),
        P("tok"),
        P("tok", "mp"),
    )
    return jax.shard_map(
        body,
        mesh=mesh,
        in_specs=placed,
        out_specs=(
            P("tok", "mp"),
            P("tok", "mp"),
            P("mp"),
            P("mp"),
            P("tok", "mp"),
            P("tok", "mp"),
            P("tok", "mp"),
        ),
        check_vma=False,
    )
```

profile of v0, /device:TPU:1, one launch (start us, length us, event | category | flops | bytes accessed | tf_op | source)
XLA Modules:
  0.0 233.1 jit_solution(3055635269094535712)
XLA Ops:
  10.0 8.4 %all-to-all-start = ((f32[16,48,256]{2,1,0:T(8,128)}), f32[16,48,256]{2,1,0:T(8,128)S(1)}, u32[]{:S(2)}, u32[]{:S(2)}) async-start(f32[16,48,256]{2,1,0:T(8,128)} %broadcast_in_dim.12), calls=%async_computation | async-start | bytes 1572864 | tf_op jit(solution)/shard_map/all_to_all | solution.py:17
  19.2 12.5 %all-to-all-done = f32[16,48,256]{2,1,0:T(8,128)S(1)} async-done(((f32[16,48,256]{2,1,0:T(8,128)}), f32[16,48,256]{2,1,0:T(8,128)S(1)}, u32[]{:S(2)}, u32[]{:S(2)}) %all-to-all-start) | async-done | bytes 786464 | tf_op jit(solution)/shard_map/all_to_all | solution.py:17
  32.2 1.3 broadcast_in_dim.14
  33.5 6.8 %all-to-all-start.1 = ((bf16[8,384,256]{1,2,0:T(8,128)(2,1)}), bf16[8,384,256]{1,2,0:T(8,128)(2,1)S(1)}, u32[]{:S(2)}, u32[]{:S(2)}) async-start(bf16[8,384,256]{1,2,0:T(8,128)(2,1)} %broadcast_in_dim.14), calls=%async_computation.1 | async-start | bytes 3145728 | tf_op jit(solution)/shard_map/all_to_all | solution.py:17
  40.5 20.4 %all-to-all-done.1 = bf16[8,384,256]{1,2,0:T(8,128)(2,1)S(1)} async-done(((bf16[8,384,256]{1,2,0:T(8,128)(2,1)}), bf16[8,384,256]{1,2,0:T(8,128)(2,1)S(1)}, u32[]{:S(2)}, u32[]{:S(2)}) %all-to-all-start.1) | async-done | bytes 1572896 | tf_op jit(solution)/shard_map/all_to_all | solution.py:17
  60.9 1.3 broadcast_in_dim.15
  62.2 4.5 %all-to-all-start.3 = ((bf16[8,384,256]{1,2,0:T(8,128)(2,1)}), bf16[8,384,256]{1,2,0:T(8,128)(2,1)S(1)}, u32[]{:S(2)}, u32[]{:S(2)}) async-start(bf16[8,384,256]{1,2,0:T(8,128)(2,1)} %broadcast_in_dim.15), calls=%async_computation.3 | async-start | bytes 3145728 | tf_op jit(solution)/shard_map/all_to_all | solution.py:17
  66.7 5.3 %fusion.33 = f32[384,1024]{1,0:T(8,128)} fusion(bf16[384,2048]{0,1:T(8,128)(2,1)S(1)} %bitcast.63, bf16[2048,1024]{1,0:T(8,128)(2,1)} %param.12), kind=kOutput, calls=%fused_computation.56 | convolution fusion | flops 1610612736 | bytes 7340032 | tf_op jit(solution)/shard_map/dot_general | solution.py:90
  72.0 3.0 %fusion.32 = f32[384,1024]{1,0:T(8,128)} fusion(bf16[384,2048]{0,1:T(8,128)(2,1)S(1)} %bitcast.64, bf16[2048,1024]{1,0:T(8,128)(2,1)S(1)} %copy-done.12), kind=kOutput, calls=%fused_computation.55 | convolution fusion | flops 1610612736 | bytes 7340032 | tf_op jit(solution)/shard_map/dot_general | solution.py:89
  75.0 12.3 %all-to-all-done.3 = bf16[8,384,256]{1,2,0:T(8,128)(2,1)S(1)} async-done(((bf16[8,384,256]{1,2,0:T(8,128)(2,1)}), bf16[8,384,256]{1,2,0:T(8,128)(2,1)S(1)}, u32[]{:S(2)}, u32[]{:S(2)}) %all-to-all-start.3) | async-done | bytes 1572896 | tf_op jit(solution)/shard_map/all_to_all | solution.py:17
  87.3 5.5 %multiply_convert_fusion = (bf16[384,1024]{1,0:T(8,128)(2,1)S(1)}, bf16[384,1024]{1,0:T(8,128)(2,1)S(1)}, bf16[384,1024]{1,0:T(8,128)(2,1)S(1)}) fusion(f32[384,1024]{1,0:T(8,128)} %fusion.32, f32[384,1024]{1,0:T(8,128)} %fusion.33, bf16[384,2048]{0,1:T(8,128)(2,1)S(1)} %bitcast.66, bf16[2048,1024]{1,0:T(8,128)(2,1)} %param.13), kind=kOutput, calls=%fused_computation.12 | convolution fusion | flops 1616904192 | bytes 11272192 | tf_op jit(solution)/shard_map/dot_general | solution.py:96
  92.9 2.4 %convert_bitcast_fusion = bf16[2048,1024]{0,1:T(8,128)(2,1)S(1)} fusion(bf16[384,1024]{1,0:T(8,128)(2,1)S(1)} %get-tuple-element.39, bf16[384,2048]{0,1:T(8,128)(2,1)S(1)} %bitcast.67), kind=kOutput, calls=%fused_computation.2 | convolution fusion | flops 1612709888 | bytes 6553600 | tf_op jit(solution)/shard_map/dot_general | solution.py:63
  95.3 5.1 %convolution_convert_fusion = bf16[2048,2048]{0,1:T(8,128)(2,1)S(1)} fusion(bf16[384,2048]{0,1:T(8,128)(2,1)S(1)} %bitcast.65, bf16[384,1024]{1,0:T(8,128)(2,1)S(1)} %get-tuple-element.37, bf16[384,1024]{1,0:T(8,128)(2,1)S(1)} %get-tuple-element.38), kind=kOutput, calls=%fused_computation.1 | convolution fusion | flops 3228565504 | bytes 11534336 | tf_op jit(solution)/shard_map/dot_general | solution.py:63
  100.4 14.4 %pad_maximum_fusion = bf16[2048,3072]{0,1:T(8,128)(2,1)} fusion(bf16[2048,1024]{0,1:T(8,128)(2,1)S(1)} %convert_bitcast_fusion, bf16[2048,2048]{0,1:T(8,128)(2,1)S(1)} %convolution_convert_fusion), kind=kLoop, calls=%fused_computation | loop fusion | flops 25165824 | bytes 25165824 | tf_op jit(solution)/shard_map/concatenate | solution.py:114
  114.7 16.6 %copy.37 = bf16[2048,3072]{1,0:T(8,128)(2,1)} copy(bf16[2048,3072]{0,1:T(8,128)(2,1)} %pad_maximum_fusion) | data formatting | bytes 25165824
  131.4 1.1 copy-done.15
  132.5 4.2 %fusion.34 = f32[384,2048]{1,0:T(8,128)S(1)} fusion(bf16[384,1024]{1,0:T(8,128)(2,1)S(1)} %copy-done.15, bf16[2048,1024]{1,0:T(8,128)(2,1)} %param.11), kind=kOutput, calls=%fused_computation.57 | convolution fusion | flops 1610612736 | bytes 8126464 | tf_op jit(solution)/shard_map/dot_general | solution.py:69
  136.7 1.8 add_convert_fusion
  138.5 1.3 copy.43
  139.8 4.6 %all-to-all-start.4 = ((bf16[8,384,256]{2,1,0:T(8,128)(2,1)}), bf16[8,384,256]{2,1,0:T(8,128)(2,1)S(1)}, u32[]{:S(2)}, u32[]{:S(2)}) async-start(bf16[8,384,256]{2,1,0:T(8,128)(2,1)} %bitcast.60), calls=%async_computation.4 | async-start | bytes 3145728 | tf_op jit(solution)/shard_map/all_to_all | solution.py:42
  144.4 4.1 %convolution_convert_fusion.1 = bf16[384,2048]{1,0:T(8,128)(2,1)S(1)} fusion(bf16[384,1024]{1,0:T(8,128)(2,1)S(1)} %copy-done.17, bf16[2048,1024]{1,0:T(8,128)(2,1)} %param.13), kind=kOutput, calls=%fused_computation.6 | convolution fusion | flops 1611399168 | bytes 6553600 | tf_op jit(solution)/shard_map/dot_general | solution.py:69
  148.5 1.2 copy.44
  149.8 15.3 %all-to-all-done.4 = bf16[8,384,256]{2,1,0:T(8,128)(2,1)S(1)} async-done(((bf16[8,384,256]{2,1,0:T(8,128)(2,1)}), bf16[8,384,256]{2,1,0:T(8,128)(2,1)S(1)}, u32[]{:S(2)}, u32[]{:S(2)}) %all-to-all-start.4) | async-done | bytes 1572896 | tf_op jit(solution)/shard_map/all_to_all | solution.py:42
  165.0 4.6 %all-to-all-start.2 = ((bf16[8,384,256]{2,1,0:T(8,128)(2,1)}), bf16[8,384,256]{2,1,0:T(8,128)(2,1)S(1)}, u32[]{:S(2)}, u32[]{:S(2)}) async-start(bf16[8,384,256]{2,1,0:T(8,128)(2,1)} %bitcast.62), calls=%async_computation.2 | async-start | bytes 3145728 | tf_op jit(solution)/shard_map/all_to_all | solution.py:42
  170.8 19.4 %all-to-all-done.2 = bf16[8,384,256]{2,1,0:T(8,128)(2,1)S(1)} async-done(((bf16[8,384,256]{2,1,0:T(8,128)(2,1)}), bf16[8,384,256]{2,1,0:T(8,128)(2,1)S(1)}, u32[]{:S(2)}, u32[]{:S(2)}) %all-to-all-start.2) | async-done | bytes 1572896 | tf_op jit(solution)/shard_map/all_to_all | solution.py:42
  191.0 3.7 %all-to-all-start.5 = ((bf16[16,48,256]{2,1,0:T(8,128)(2,1)}), bf16[16,48,256]{2,1,0:T(8,128)(2,1)S(1)}, u32[]{:S(2)}, u32[]{:S(2)}) async-start(bf16[16,48,256]{2,1,0:T(8,128)(2,1)} %broadcast_in_dim.16), calls=%async_computation.5 | async-start | bytes 786432 | tf_op jit(solution)/shard_map/all_to_all | solution.py:17
  195.5 8.4 %all-to-all-done.5 = bf16[16,48,256]{2,1,0:T(8,128)(2,1)S(1)} async-done(((bf16[16,48,256]{2,1,0:T(8,128)(2,1)}), bf16[16,48,256]{2,1,0:T(8,128)(2,1)S(1)}, u32[]{:S(2)}, u32[]{:S(2)}) %all-to-all-start.5) | async-done | bytes 393248 | tf_op jit(solution)/shard_map/all_to_all | solution.py:17
  205.7 15.9 %reduce-scatter.4.cloned.1.call-done = bf16[128,3072]{1,0:T(8,128)(2,1)} async-done(((bf16[2048,3072]{1,0:T(8,128)(2,1)}), bf16[128,3072]{1,0:T(8,128)(2,1)}) %reduce-scatter.4.cloned.1.call-update) | async-done | bytes 786448
  221.7 1.5 copy.38
  223.3 1.0 copy.36
  224.3 1.0 copy.35
  225.3 1.0 copy.34
  (63 shorter events, 8.9 us)
Async XLA Ops:
  9.0 22.7 %copy-start.10 = (s32[24]{0:T(128)S(1)}, s32[24]{0:T(128)}, u32[]{:S(2)}) copy-start(s32[24]{0:T(128)} %param.14) | copy-start | bytes 292
  9.0 22.9 %copy-start = (bf16[384,256]{1,0:T(8,128)(2,1)S(1)}, bf16[384,256]{1,0:T(8,128)(2,1)}, u32[]{:S(2)}) copy-start(bf16[384,256]{1,0:T(8,128)(2,1)} %param.8) | copy-start | bytes 589828
  10.0 21.7 %all-to-all-start = ((f32[16,48,256]{2,1,0:T(8,128)}), f32[16,48,256]{2,1,0:T(8,128)S(1)}, u32[]{:S(2)}, u32[]{:S(2)}) async-start(f32[16,48,256]{2,1,0:T(8,128)} %broadcast_in_dim.12), calls=%async_computation | async-start | bytes 1572864 | tf_op jit(solution)/shard_map/all_to_all | solution.py:17
  31.7 1.8 copy-start.5
  31.9 1.6 copy-start.7
  33.5 6.8 %copy-start.3 = (bf16[384,256]{1,0:T(8,128)(2,1)S(1)}, bf16[384,256]{1,0:T(8,128)(2,1)}, u32[]{:S(2)}) copy-start(bf16[384,256]{1,0:T(8,128)(2,1)} %param.15) | copy-start | bytes 589828
  33.5 27.4 %all-to-all-start.1 = ((bf16[8,384,256]{1,2,0:T(8,128)(2,1)}), bf16[8,384,256]{1,2,0:T(8,128)(2,1)S(1)}, u32[]{:S(2)}, u32[]{:S(2)}) async-start(bf16[8,384,256]{1,2,0:T(8,128)(2,1)} %broadcast_in_dim.14), calls=%async_computation.1 | async-start | bytes 3145728 | tf_op jit(solution)/shard_map/all_to_all | solution.py:17
  62.2 25.1 %all-to-all-start.3 = ((bf16[8,384,256]{1,2,0:T(8,128)(2,1)}), bf16[8,384,256]{1,2,0:T(8,128)(2,1)S(1)}, u32[]{:S(2)}, u32[]{:S(2)}) async-start(bf16[8,384,256]{1,2,0:T(8,128)(2,1)} %broadcast_in_dim.15), calls=%async_computation.3 | async-start | bytes 3145728 | tf_op jit(solution)/shard_map/all_to_all | solution.py:17
  66.7 155.0 %reduce-scatter.4.cloned.1.call-start = ((), (), s32[]{:S(2)}) async-start(), calls=%async_computation.7 | async-start | bytes 13369344
  66.7 5.4 %copy-start.12 = (bf16[2048,1024]{1,0:T(8,128)(2,1)S(1)}, bf16[2048,1024]{1,0:T(8,128)(2,1)}, u32[]{:S(2)}) copy-start(bf16[2048,1024]{1,0:T(8,128)(2,1)} %param.11) | copy-start | bytes 12582916
  92.8 2.4 %copy-start.16 = (bf16[384,1024]{1,0:T(8,128)(2,1)}, bf16[384,1024]{1,0:T(8,128)(2,1)S(1)}, u32[]{:S(2)}) copy-start(bf16[384,1024]{1,0:T(8,128)(2,1)S(1)} %get-tuple-element.39) | copy-start | bytes 2359300
  92.8 2.4 %copy-start.14 = (bf16[384,1024]{1,0:T(8,128)(2,1)}, bf16[384,1024]{1,0:T(8,128)(2,1)S(1)}, u32[]{:S(2)}) copy-start(bf16[384,1024]{1,0:T(8,128)(2,1)S(1)} %get-tuple-element.38) | copy-start | bytes 2359300
  92.8 2.4 %copy-start.18 = (bf16[384,1024]{1,0:T(8,128)(2,1)}, bf16[384,1024]{1,0:T(8,128)(2,1)S(1)}, u32[]{:S(2)}) copy-start(bf16[384,1024]{1,0:T(8,128)(2,1)S(1)} %get-tuple-element.37) | copy-start | bytes 2359300
  131.3 1.1 copy-start.15
  132.5 4.2 %copy-start.13 = (bf16[2048,1024]{1,0:T(8,128)(2,1)S(1)}, bf16[2048,1024]{1,0:T(8,128)(2,1)}, u32[]{:S(2)}) copy-start(bf16[2048,1024]{1,0:T(8,128)(2,1)} %param.12) | copy-start | bytes 12582916
  132.5 4.2 %copy-start.19 = (bf16[384,1024]{1,0:T(8,128)(2,1)S(1)}, bf16[384,1024]{1,0:T(8,128)(2,1)}, u32[]{:S(2)}) copy-start(bf16[384,1024]{1,0:T(8,128)(2,1)} %copy-done.18) | copy-start | bytes 2359300
  139.8 4.6 %copy-start.17 = (bf16[384,1024]{1,0:T(8,128)(2,1)S(1)}, bf16[384,1024]{1,0:T(8,128)(2,1)}, u32[]{:S(2)}) copy-start(bf16[384,1024]{1,0:T(8,128)(2,1)} %copy-done.16) | copy-start | bytes 2359300
  139.8 25.2 %all-to-all-start.4 = ((bf16[8,384,256]{2,1,0:T(8,128)(2,1)}), bf16[8,384,256]{2,1,0:T(8,128)(2,1)S(1)}, u32[]{:S(2)}, u32[]{:S(2)}) async-start(bf16[8,384,256]{2,1,0:T(8,128)(2,1)} %bitcast.60), calls=%async_computation.4 | async-start | bytes 3145728 | tf_op jit(solution)/shard_map/all_to_all | solution.py:42
  165.0 4.6 %copy-start.6 = (f32[48,256]{1,0:T(8,128)S(1)}, f32[48,256]{1,0:T(8,128)}, u32[]{:S(2)}) copy-start(f32[48,256]{1,0:T(8,128)} %copy-done.5) | copy-start | bytes 147460
  165.0 25.2 %all-to-all-start.2 = ((bf16[8,384,256]{2,1,0:T(8,128)(2,1)}), bf16[8,384,256]{2,1,0:T(8,128)(2,1)S(1)}, u32[]{:S(2)}, u32[]{:S(2)}) async-start(bf16[8,384,256]{2,1,0:T(8,128)(2,1)} %bitcast.62), calls=%async_computation.2 | async-start | bytes 3145728 | tf_op jit(solution)/shard_map/all_to_all | solution.py:42
  169.6 0.9 copy-start.1
  169.6 0.9 copy-start.8
  170.5 24.2 %copy-start.11 = (f32[256]{0:T(256)S(1)}, f32[256]{0:T(256)}, u32[]{:S(2)}) copy-start(f32[256]{0:T(256)} %param.10) | copy-start | bytes 3076
  191.0 13.8 %copy-start.2 = (bf16[384,256]{1,0:T(8,128)(2,1)S(1)}, bf16[384,256]{1,0:T(8,128)(2,1)}, u32[]{:S(2)}) copy-start(bf16[384,256]{1,0:T(8,128)(2,1)} %param.8) | copy-start | bytes 589828
  191.0 13.8 %copy-start.4 = (bf16[384,256]{1,0:T(8,128)(2,1)S(1)}, bf16[384,256]{1,0:T(8,128)(2,1)}, u32[]{:S(2)}) copy-start(bf16[384,256]{1,0:T(8,128)(2,1)} %param.15) | copy-start | bytes 589828
  191.0 13.8 %copy-start.9 = (f32[24,256]{1,0:T(8,128)S(1)}, f32[24,256]{1,0:T(8,128)}, u32[]{:S(2)}) copy-start(f32[24,256]{1,0:T(8,128)} %copy-done.7) | copy-start | bytes 73732
  191.0 12.9 %all-to-all-start.5 = ((bf16[16,48,256]{2,1,0:T(8,128)(2,1)}), bf16[16,48,256]{2,1,0:T(8,128)(2,1)S(1)}, u32[]{:S(2)}, u32[]{:S(2)}) async-start(bf16[16,48,256]{2,1,0:T(8,128)(2,1)} %broadcast_in_dim.16), calls=%async_computation.5 | async-start | bytes 786432 | tf_op jit(solution)/shard_map/all_to_all | solution.py:17
Sparse Core Ops, SparseCore 0:
  131.5 90.1 reduce-scatter.3
where the time goes:
time: 234 us; the launch traced here: 233 us
  waiting for transfers between devices  104 us (44%)
  matrix products  32.8 us (14%)
  starting transfers between devices  32.6 us (14%)
  local copies, waits for them, and re-layouts  31 us (13%)
  other arithmetic  18.2 us (8%)
  between operations  14.3 us (6%)
    all_to_all x4, waiting for transfers between devices, from_everyone(): return lax.all_to_all(copies, axis, split_axis=0, concat_axis=0, tiled=True)  53.5 us
    all_to_all x2, waiting for transfers between devices, sent_and_summed(): pieces = lax.all_to_all(split_up(x, dim, count), axis, 0, 0, tiled=True)  34.7 us
    all_to_all x4, starting transfers between devices, from_everyone(): return lax.all_to_all(copies, axis, split_axis=0, concat_axis=0, tiled=True)  23.4 us
    unnamed x46, local copies, waits for them, and re-layouts  23.1 us
    unnamed x2, waiting for transfers between devices  16 us
    concatenate x1, other arithmetic, body(): jnp.concatenate([upper, lower], axis=1).astype(jnp.bfloat16)  14.4 us
    dot_general x3, matrix products, contract_cols(): lax.dot_general(left, right, (((1,), (1,)), ((), ())), preferred_element_...  10.1 us
    all_to_all x2, starting transfers between devices, sent_and_summed(): pieces = lax.all_to_all(split_up(x, dim, count), axis, 0, 0, tiled=True)  9.19 us
  transfers between devices with their start and end apart: 7, of which 7 were waited for; matrix products, arithmetic and copies ran while one was open for 11% of the time, Pallas kernels for 0%

commit v1 on v0

v1 whole, which is shorter than its diff:
```python
import jax
import jax.numpy as jnp
from jax import lax
from jax.experimental import pallas as pl
from jax.experimental.pallas import tpu as pltpu
from jax.sharding import Mesh
from jax.sharding import PartitionSpec as P


GHOST = 128
BLK = 16
RING = 4
NEAR = [(i, i ^ 1) for i in range(RING)]
FAR = [(i, RING - 1 - i) for i in range(RING)]
CORES = [(0, 1), (1, 0)]
EPSILON = 1e-05
MOMENTUM = 0.1


bf16 = jnp.bfloat16
f32 = jnp.float32


PATTERNS = (("z", 0), ("z", 1), ("x", 0), ("x", 1))


def halving(i, first):
    near, far = i ^ 1, RING - 1 - i
    p, q = (near, far) if first == 0 else (far, near)
    return [RING - 1 - p if first == 0 else p ^ 1, p, q, i]


def row_blocks(coords, pattern):
    major, first = pattern
    hz, hx = halving(coords[0], first), halving(coords[1], first)
    if major == "z":
        return [RING * a + b for a in hz for b in hx]
    return [RING * a + b for b in hx for a in hz]


def feature_blocks(coords, other):
    core = coords[3] if other == 0 else 1 - coords[3]
    return [2 * ((coords[2] + k) & (RING - 1)) + core for k in range(RING)]


def shift(k):
    return [(i, (i + k) % RING) for i in range(RING)]


def to_all(x):
    return lax.all_to_all(x, ("z", "x"), 0, 0, tiled=True)


def vmem_spec():
    return pl.BlockSpec(memory_space=pltpu.VMEM)


def smem_spec():
    return pl.BlockSpec(memory_space=pltpu.SMEM)


def gathered(x):
    near = [x]
    for k in (1, 3, 2):
        near.append(lax.ppermute(x, "y", shift(-k)))
    near = [near[0], near[1], near[3], near[2]]
    far = []
    for k in range(RING):
        far.append(lax.ppermute(near[k], "c", CORES))
    return near + far


def block_sum(value):
    return jnp.sum(value, axis=0, keepdims=True)


def spread(acc, out):
    table = acc[...].astype(bf16)
    for i in range(out.shape[0]):
        out[i] = table


def own_gain(coords, gain, feat):
    return gain[:, pl.ds(pl.multiple_of((2 * coords[2] + coords[3]) * feat, feat), feat)]


def received_sum(received):
    total = received[0].astype(f32)
    for i in range(1, received.shape[0]):
        total = total + received[i].astype(f32)
    return total


def stats_kernel(groups, tokens, out, acc):
    acc[...] = jnp.zeros_like(acc)
    for b in range(tokens.shape[0] // BLK):
        value = tokens[b * BLK : (b + 1) * BLK, :].astype(f32)
        row = pl.ds(groups[b], 1)
        acc[row, :] = acc[row, :] + block_sum(value * value)
    spread(acc, out)


def stats(groups, tokens, groups_total):
    feat = tokens.shape[1]
    return pl.pallas_call(
        stats_kernel,
        out_shape=jax.ShapeDtypeStruct((RING * RING, groups_total, feat), bf16),
        in_specs=[smem_spec(), vmem_spec()],
        out_specs=vmem_spec(),
        scratch_shapes=[pltpu.VMEM((groups_total, feat), f32)],
        compiler_params=limits(4),
        name="stats",
    )(groups, tokens)


def norm_kernel(groups, coords, tokens, gain, running, received, hid, table, running_new):
    quad_mean = received_sum(received) * (1.0 / GHOST)
    table[...] = lax.rsqrt(quad_mean + EPSILON)
    mean = jnp.sum(quad_mean, axis=0, keepdims=True) / quad_mean.shape[0]
    running_new[...] = (1.0 - MOMENTUM) * running[...] + MOMENTUM * mean
    gain_row = own_gain(coords, gain, tokens.shape[1])
    for b in range(tokens.shape[0] // BLK):
        rows = slice(b * BLK, (b + 1) * BLK)
        scale = table[pl.ds(groups[b], 1), :]
        hid[rows, :] = (gain_row * (tokens[rows, :].astype(f32) * scale)).astype(bf16)


def normalized(groups, coords, tokens, gain, running, received):
    groups_total = received.shape[1]
    rows, feat = tokens.shape
    return pl.pallas_call(
        norm_kernel,
        out_shape=(
            jax.ShapeDtypeStruct((rows, feat), bf16),
            jax.ShapeDtypeStruct((groups_total, feat), f32),
            jax.ShapeDtypeStruct((1, feat), f32),
        ),
        in_specs=[smem_spec(), smem_spec()] + [vmem_spec()] * 4,
        out_specs=(vmem_spec(),) * 3,
        compiler_params=limits(4),
        name="normalized",
    )(groups, coords, tokens, gain, running, received)


def partial_kernel(groups, tokens, table, own, *refs):
    came, (grad, out, acc) = refs[:-3], refs[-3:]
    total = own[...]
    for ref in came:
        total = total + ref[...].astype(f32)
    grad[...] = total.T
    acc[...] = jnp.zeros_like(acc)
    for b in range(tokens.shape[0] // BLK):
        rows = slice(b * BLK, (b + 1) * BLK)
        row = pl.ds(groups[b], 1)
        normed = tokens[rows, :].astype(f32) * table[row, :]
        acc[row, :] = acc[row, :] + block_sum(grad[rows, :] * normed)
    spread(acc, out)


def partials(groups, tokens, table, own, came):
    rows, feat = tokens.shape
    return pl.pallas_call(
        partial_kernel,
        out_shape=(
            jax.ShapeDtypeStruct((rows, feat), f32),
            jax.ShapeDtypeStruct((RING * RING, *table.shape), bf16),
        ),
        in_specs=[smem_spec()] + [vmem_spec()] * (3 + len(came)),
        out_specs=(vmem_spec(),) * 2,
        scratch_shapes=[pltpu.VMEM(table.shape, f32)],
        compiler_params=limits(6),
        name="partials",
    )(groups, tokens, table, own, *came)


def input_kernel(groups, coords, tokens, cotangent, gain, table, grad, received, out, grad_gain, acc):
    partial = received_sum(received)
    grad_gain[...] = jnp.sum(partial, axis=0, keepdims=True)
    gain_row = own_gain(coords, gain, tokens.shape[1])
    acc[...] = gain_row * partial * (1.0 / GHOST)
    for b in range(tokens.shape[0] // BLK):
        rows = slice(b * BLK, (b + 1) * BLK)
        row = pl.ds(groups[b], 1)
        scale = table[row, :]
        normed = tokens[rows, :].astype(f32) * scale
        inner = gain_row * grad[rows, :] - normed * acc[row, :]
        out[rows, :] = (cotangent[rows, :].astype(f32) + scale * inner).astype(bf16)


def input_grads(groups, coords, tokens, cotangent, gain, table, grad, received):
    rows, feat = tokens.shape
    return pl.pallas_call(
        input_kernel,
        out_shape=(
            jax.ShapeDtypeStruct((rows, feat), bf16),
            jax.ShapeDtypeStruct((1, feat), f32),
        ),
        in_specs=[smem_spec(), smem_spec()] + [vmem_spec()] * 6,
        out_specs=(vmem_spec(),) * 2,
        scratch_shapes=[pltpu.VMEM(table.shape, f32)],
        compiler_params=limits(6),
        name="input_grads",
    )(groups, coords, tokens, cotangent, gain, table, grad, received)


def branch_kernel(tokens, own, *refs):
    came, out = refs[:-1], refs[-1]
    total = own[...]
    for ref in came:
        total = total + ref[...].astype(f32)
    out[...] = (tokens[...].astype(f32) + total.T).astype(bf16)


def branch_out(tokens, own, came):
    return pl.pallas_call(
        branch_kernel,
        out_shape=jax.ShapeDtypeStruct(tokens.shape, bf16),
        in_specs=[vmem_spec()] * (2 + len(came)),
        out_specs=vmem_spec(),
        compiler_params=limits(6),
        name="branch_out",
    )(tokens, own, *came)


def grad_kernel(dy, weight, out):
    out[...] = jnp.dot(dy[...], weight[...], preferred_element_type=f32)


def hidden_grads(dy, weight):
    rows, width = dy.shape
    hidden = weight.shape[1]
    part = hidden // RING
    return pl.pallas_call(
        grad_kernel,
        grid=(RING,),
        out_shape=jax.ShapeDtypeStruct((rows, hidden), f32),
        in_specs=[
            pl.BlockSpec((rows, width), lambda i: (0, 0)),
            pl.BlockSpec((width, part), lambda i: (0, i)),
        ],
        out_specs=pl.BlockSpec((rows, part), lambda i: (0, i)),
        compiler_params=limits(12),
        name="hidden_grads",
    )(dy, weight)


def limits(mib):
    return pltpu.CompilerParams(vmem_limit_bytes=mib << 20)


def assemble_kernel(coords, *refs):
    pieces, (out, turned) = refs[:-2], refs[-2:]
    width = pieces[0].shape[1]
    places = feature_blocks(coords, 0) + feature_blocks(coords, 1)
    for place, piece in zip(places, pieces):
        first = pl.multiple_of(place * width, width)
        out[:, pl.ds(first, width)] = piece[...]
        turned[pl.ds(first, width), :] = piece[...].T


def assembled(coords, pieces):
    rows, width = pieces[0].shape
    total = width * len(pieces)
    return pl.pallas_call(
        assemble_kernel,
        out_shape=(
            jax.ShapeDtypeStruct((rows, total), bf16),
            jax.ShapeDtypeStruct((total, rows), bf16),
        ),
        in_specs=[smem_spec()] + [vmem_spec()] * len(pieces),
        out_specs=(vmem_spec(), vmem_spec()),
        compiler_params=limits(10),
        name="assemble",
    )(coords, *pieces)


def rows_product(blocks, turned, right, send, keep, first):
    columns = slice(first, first + right.shape[1])
    half = len(blocks) // 2
    for part, out in ((blocks[:half], send), (blocks[half:], keep)):
        left = jnp.concatenate(
            [turned[pl.ds(pl.multiple_of(b * 128, 128), 128), :] for b in part], axis=0
        )
        out[:, columns] = jnp.dot(left, right, preferred_element_type=f32).astype(out.dtype)


def hidden_kernel(pattern):
    def kernel(coords, hid, hid_t, dy_t, grad_in, gate_w, up_w, hidden_t, ggi_t, gl_t, send, keep):
        gate = jnp.dot(hid[...], gate_w[...], preferred_element_type=f32)
        lift = jnp.dot(hid[...], up_w[...], preferred_element_type=f32)
        grad = grad_in[...]
        sigma = jax.nn.sigmoid(gate)
        act = gate * sigma
        hidden = (act * lift).astype(bf16)
        ggi = (grad * lift * sigma * (1.0 + gate * (1.0 - sigma))).astype(bf16)
        gl = (grad * act).astype(bf16)
        part = gate.shape[1]
        blocks = row_blocks(coords, pattern)
        rows_product(blocks, dy_t, hidden, send, keep, 0)
        rows_product(blocks, hid_t, jnp.concatenate([ggi, gl], axis=1), send, keep, part)
        hidden_t[...] = hidden.T
        ggi_t[...] = ggi.T
        gl_t[...] = gl.T

    return kernel


def hidden_part(p, coords, hid, hid_t, dy_t, grad_in, gate_w, up_w):
    rows, width = hid.shape
    part = gate_w.shape[1] // RING

    def fixed(*shape):
        return pl.BlockSpec(shape, lambda i: (0, 0))

    weight = pl.BlockSpec((width, part), lambda i: (0, p))
    act = jax.ShapeDtypeStruct((part, rows), bf16)
    half = jax.ShapeDtypeStruct((width // 2, 3 * part), bf16)
    return pl.pallas_call(
        hidden_kernel(PATTERNS[p]),
        grid=(1,),
        out_shape=(act, act, act, half, half),
        in_specs=[
            smem_spec(),
            fixed(rows, width),
            fixed(width, rows),
            fixed(width, rows),
            pl.BlockSpec((rows, part), lambda i: (0, p)),
            weight,
            weight,
        ],
        out_specs=(fixed(part, rows),) * 3 + (fixed(width // 2, 3 * part),) * 2,
        compiler_params=limits(20),
        name="hidden_part",
    )(coords, hid, hid_t, dy_t, grad_in, gate_w, up_w)


def back_kernel(pairs):
    def kernel(coords, *refs):
        acts = refs[: pairs * RING]
        weights = refs[pairs * RING : pairs * RING + pairs]
        outs = refs[pairs * RING + pairs :]
        feat = outs[0].shape[1]
        for other, out in ((1, outs[0]), (0, outs[1])):
            total = None
            for j in range(pairs):
                act = jnp.concatenate([r[...] for r in acts[j * RING : (j + 1) * RING]], axis=0)
                left = jnp.concatenate(
                    [
                        weights[j][pl.ds(pl.multiple_of(b * feat, feat), feat), :]
                        for b in feature_blocks(coords, other)
                    ],
                    axis=0,
                )
                term = jnp.dot(left, act, preferred_element_type=f32)
                total = term if total is None else total + term
            for k in range(RING):
                out[k] = total[k * feat : (k + 1) * feat, :].astype(bf16)

    return kernel


def back(coords, acts, weights):
    rows = acts[0][0].shape[1]
    feat = weights[0].shape[0] // (2 * RING)
    pairs = len(weights)
    out = jax.ShapeDtypeStruct((RING, feat, rows), bf16)
    return pl.pallas_call(
        back_kernel(pairs),
        in_specs=[smem_spec()] + [vmem_spec()] * (pairs * RING + pairs),
        out_specs=(vmem_spec(), vmem_spec()),
        out_shape=(out, out),
        compiler_params=limits(20),
        name="back",
    )(coords, *[a for group in acts for a in group], *weights)


def chip_sum_kernel(near, other, own, *sends):
    own[...] = near[0].astype(f32) + other[0].astype(f32)
    for k, send in enumerate(sends, 1):
        send[...] = (near[k].astype(f32) + other[k].astype(f32)).astype(bf16)


def mp_scattered(far, near):
    other = lax.ppermute(far, "c", CORES)
    piece = near.shape[1:]
    own, *sends = pl.pallas_call(
        chip_sum_kernel,
        out_shape=(jax.ShapeDtypeStruct(piece, f32),)
        + (jax.ShapeDtypeStruct(piece, bf16),) * (RING - 1),
        in_specs=[vmem_spec()] * 2,
        out_specs=(vmem_spec(),) * RING,
        compiler_params=limits(6),
        name="chip_sum",
    )(near, other)
    came = []
    for k in (1, 3, 2):
        came.append(lax.ppermute(sends[k - 1], "y", shift(k)))
    return own, came


def split_kernel(keep, came, send, kept):
    half = send.shape[0]
    send[...] = (keep[:half, :].astype(f32) + came[:half, :].astype(f32)).astype(bf16)
    kept[...] = (keep[half:, :].astype(f32) + came[half:, :].astype(f32)).astype(bf16)


def split_add(keep, came):
    half = jax.ShapeDtypeStruct((keep.shape[0] // 2, keep.shape[1]), bf16)
    return pl.pallas_call(
        split_kernel,
        out_shape=(half, half),
        in_specs=[vmem_spec()] * 2,
        out_specs=(vmem_spec(),) * 2,
        compiler_params=limits(8),
        name="split_add",
    )(keep, came)


def finish_kernel(*refs):
    ins, outs = refs[: 2 * RING], refs[2 * RING :]
    for p in range(RING):
        total = ins[2 * p][...].astype(f32) + ins[2 * p + 1][...].astype(f32)
        part = total.shape[1] // len(outs)
        for j, out in enumerate(outs):
            out[:, p * part : (p + 1) * part] = total[:, j * part : (j + 1) * part]


def finished(pairs):
    rows, width = pairs[0][0].shape
    out = jax.ShapeDtypeStruct((rows, width // 3 * RING), f32)
    return pl.pallas_call(
        finish_kernel,
        out_shape=(out,) * 3,
        in_specs=[vmem_spec()] * (2 * RING),
        out_specs=(vmem_spec(),) * 3,
        compiler_params=limits(6),
        name="finished",
    )(*[a for pair in pairs for a in pair])


def body(tokens, norm_gain, running_sq, gate_weight, up_weight, down_weight_t, groups, cotangent):
    tok_rows, feat = tokens.shape
    groups_total = tok_rows * RING * RING // GHOST
    coords = jnp.stack([lax.axis_index(a) for a in ("z", "x", "y", "c")]).astype(jnp.int32)
    gain = norm_gain.reshape(1, -1)
    local = stats(groups, tokens, groups_total)
    received = to_all(local)
    dy_pieces = gathered(cotangent)
    dy_full, dy_turned = assembled(coords, dy_pieces)
    hid, table, running_new = normalized(
        groups, coords, tokens, gain, running_sq.reshape(1, feat), received
    )
    hid_pieces = gathered(hid)
    grad_hidden = hidden_grads(dy_full, down_weight_t)
    hid_full, hid_turned = assembled(coords, hid_pieces)
    parts = []
    for p in range(RING):
        parts.append(
            hidden_part(
                p, coords, hid_full, hid_turned, dy_turned, grad_hidden, gate_weight, up_weight
            )
        )
    last = []
    for p, (major, first) in enumerate(PATTERNS):
        minor = "x" if major == "z" else "z"
        pair = (NEAR, FAR) if first == 0 else (FAR, NEAR)
        send, keep = parts[p][3:]
        for i, (axis, route) in enumerate(((major, 0), (major, 1), (minor, 0), (minor, 1)), 1):
            came = lax.ppermute(send, axis, pair[route])
            if i < 4:
                send, keep = split_add(keep, came)
        last.append((keep, came))
    grad_down_t, grad_gate, grad_up = finished(last)

    far, near = back(
        coords, [[q[1] for q in parts], [q[2] for q in parts]], [gate_weight, up_weight]
    )
    kept, came = mp_scattered(far, near)
    grad, local = partials(groups, tokens, table, kept, came)
    received = to_all(local)
    grad_tokens, grad_gain = input_grads(groups, coords, tokens, cotangent, gain, table, grad, received)

    far, near = back(coords, [[q[0] for q in parts]], [down_weight_t])
    kept, came = mp_scattered(far, near)
    block_out = branch_out(tokens, kept, came)
    return (
        block_out,
        grad_tokens,
        running_new.reshape(feat),
        grad_gain.reshape(feat),
        grad_gate,
        grad_up,
        grad_down_t,
    )


def solution(mesh):
    torus = Mesh(mesh.devices.reshape(RING, RING, RING, 2), ("z", "x", "y", "c"))
    tok, mp = ("z", "x"), ("y", "c")
    placed = (P(tok, mp), P(), P(mp), P(None, mp), P(None, mp), P(None, mp), P(tok), P(tok, mp))
    out = (P(tok, mp), P(tok, mp), P(mp), P(mp), P(tok, mp), P(tok, mp), P(tok, mp))

    return jax.shard_map(body, mesh=torus, in_specs=placed, out_specs=out, check_vma=False)
```

time: 234 us -> 171 us (0.73)
  the two profiles are of different devices: /device:TPU:1 before, /device:TPU:16 now
where the time goes in v1:
time: 171 us
  waiting for transfers between devices  60.1 us (35%)
  starting transfers between devices  55.1 us (32%)
  Pallas kernels  43 us (25%)
  local copies, waits for them, and re-layouts  11.5 us (7%)
    ppermute x16, waiting for transfers between devices, body(): came = lax.ppermute(send, axis, pair[route])  40.1 us
    ppermute x16, starting transfers between devices, body(): came = lax.ppermute(send, axis, pair[route])  21.7 us
    ppermute x6, waiting for transfers between devices, gathered(): near.append(lax.ppermute(x, 'y', shift(-k)))  15 us
    pallas_call x4, Pallas kernels, hidden_part(): pl.pallas_call(hidden_kernel(PATTERNS[p]), grid=(1,), out_shape=(act, act...  13.3 us
    all_to_all x2, starting transfers between devices, to_all(): return lax.all_to_all(x, ('z', 'x'), 0, 0, tiled=True)  12.1 us
    unnamed x56, local copies, waits for them, and re-layouts  11.5 us
    ppermute x6, starting transfers between devices, mp_scattered(): came.append(lax.ppermute(sends[k - 1], 'y', shift(k)))  11.3 us
    ppermute x6, starting transfers between devices, gathered(): near.append(lax.ppermute(x, 'y', shift(-k)))  9.27 us
  transfers between devices with their start and end apart: 40, of which 15 were waited for; matrix products, arithmetic and copies ran while one was open for 0% of the time, Pallas kernels for 21%

profile of v1, /device:TPU:16, one launch (start us, length us, event | category | flops | bytes accessed | tf_op | source)
XLA Modules:
  0.0 170.7 jit_solution(17019710325028466873)
XLA Ops:
  3.7 7.9 %all-to-all-start = ((bf16[16,48,256]{2,1,0:T(8,128)(2,1)}), bf16[16,48,256]{2,1,0:T(8,128)(2,1)S(1)}, u32[]{:S(2)}, u32[]{:S(2)}) async-start(bf16[16,48,256]{2,1,0:T(8,128)(2,1)} %stats.1), calls=%async_computation | async-start | bytes 786432 | tf_op jit(solution)/shard_map/all_to_all | solution.py:51
  12.1 2.9 %collective-permute-start.8 = (bf16[384,256]{1,0:T(8,128)(2,1)}, bf16[384,256]{1,0:T(8,128)(2,1)S(1)}, u32[]{:S(2)}, u32[]{:S(2)}) collective-permute-start(bf16[384,256]{1,0:T(8,128)(2,1)} %cotangent.1), channel_id=1, source_target_pairs={{0,4},{2,6},{4,0},{6,2},{1,5},{3,7},{5,1},{7,3},{8,12},{10,14},{12... | collective-permute-start | bytes 589832 | tf_op jit(solution)/shard_map/ppermute | solution.py:65
  15.1 4.5 %collective-permute-done.7.refs_1_ = bf16[384,256]{1,0:T(8,128)(2,1)S(1)} collective-permute-done((bf16[384,256]{1,0:T(8,128)(2,1)}, bf16[384,256]{1,0:T(8,128)(2,1)S(1)}, u32[]{:S(2)}, u32[]{:S(2)}) %collective-permute-start.7) | collective-permute-done | bytes 196640 | tf_op jit(solution)/shard_map/ppermute | solution.py:65
  25.8 2.2 %collective-permute-start = (bf16[384,256]{1,0:T(8,128)(2,1)S(1)}, bf16[384,256]{1,0:T(8,128)(2,1)S(1)}, u32[]{:S(2)}, u32[]{:S(2)}) collective-permute-start(bf16[384,256]{1,0:T(8,128)(2,1)S(1)} %get-tuple-element.77.refs_0_), channel_id=1, source_target_pairs={{0,6},{2,0},{4,2},{6,4},{1,7},{3,1},{5,3},{7,5},{8,14},{10,8},{12,... | collective-permute-start | bytes 589832 | tf_op jit(solution)/shard_map/ppermute | solution.py:65
  28.0 3.6 %collective-permute-start.1 = (bf16[384,256]{1,0:T(8,128)(2,1)S(1)}, bf16[384,256]{1,0:T(8,128)(2,1)S(1)}, u32[]{:S(2)}, u32[]{:S(2)}) collective-permute-start(bf16[384,256]{1,0:T(8,128)(2,1)S(1)} %get-tuple-element.77.refs_0_), channel_id=1, source_target_pairs={{0,4},{2,6},{4,0},{6,2},{1,5},{3,7},{5,1},{7,3},{8,12},{10,14},{12... | collective-permute-start | bytes 589832 | tf_op jit(solution)/shard_map/ppermute | solution.py:65
  32.2 3.1 %collective-permute-done.refs_1_ = bf16[384,256]{1,0:T(8,128)(2,1)S(1)} collective-permute-done((bf16[384,256]{1,0:T(8,128)(2,1)S(1)}, bf16[384,256]{1,0:T(8,128)(2,1)S(1)}, u32[]{:S(2)}, u32[]{:S(2)}) %collective-permute-start) | collective-permute-done | bytes 196640 | tf_op jit(solution)/shard_map/ppermute | solution.py:65
  35.3 2.1 %collective-permute-done.1.refs_2_ = bf16[384,256]{1,0:T(8,128)(2,1)S(1)} collective-permute-done((bf16[384,256]{1,0:T(8,128)(2,1)S(1)}, bf16[384,256]{1,0:T(8,128)(2,1)S(1)}, u32[]{:S(2)}, u32[]{:S(2)}) %collective-permute-start.1) | collective-permute-done | bytes 196640 | tf_op jit(solution)/shard_map/ppermute | solution.py:65
  37.4 3.3 %collective-permute-done.2.refs_3_ = bf16[384,256]{1,0:T(8,128)(2,1)S(1)} collective-permute-done((bf16[384,256]{1,0:T(8,128)(2,1)S(1)}, bf16[384,256]{1,0:T(8,128)(2,1)S(1)}, u32[]{:S(2)}, u32[]{:S(2)}) %collective-permute-start.2) | collective-permute-done | bytes 196640 | tf_op jit(solution)/shard_map/ppermute | solution.py:65
  42.0 2.2 %copy-done.2 = bf16[2048,1024]{1,0:T(8,128)(2,1)S(1)} copy-done((bf16[2048,1024]{1,0:T(8,128)(2,1)S(1)}, bf16[2048,1024]{1,0:T(8,128)(2,1)}, u32[]{:S(2)}) %copy-start.2) | copy-done | bytes 4194328
  44.2 3.0 %hidden_grads.1.grad_in = f32[384,1024]{1,0:T(8,128)S(1)} custom-call(bf16[384,2048]{1,0:T(8,128)(2,1)S(1)} %get-tuple-element.81.dy, bf16[2048,1024]{1,0:T(8,128)(2,1)S(1)} %copy-done.2), custom_call_target="tpu_custom_call" | custom-call | tf_op jit(solution)/shard_map/hidden_grads/pallas_call | solution.py:233
  48.5 3.3 %hidden_part.7 = (bf16[256,384]{1,0:T(8,128)(2,1)S(1)}, bf16[256,384]{1,0:T(8,128)(2,1)S(1)}, bf16[256,384]{1,0:T(8,128)(2,1)S(1)}, bf16[1024,768]{1,0:T(8,128)(2,1)S(1)}, bf16[1024,768]{1,0:T(8,128)(2,1)S(1)}) custom-call(s32[4]{0:T(128)S(1)} %pad_add_fusion.coords, bf16[384,2048]{1,0:T(8,128)(2,1)S(1)} %get-tuple-element.78.hid, ...), custom_call_target="tpu_custom_call" | custom-call | tf_op jit(solution)/shard_map/hidden_part/pallas_call | solution.py:318
  51.9 2.9 %collective-permute-start.34 = (bf16[1024,768]{1,0:T(8,128)(2,1)S(1)}, bf16[1024,768]{1,0:T(8,128)(2,1)S(1)}, u32[]{:S(2)}, u32[]{:S(2)}) collective-permute-start(bf16[1024,768]{1,0:T(8,128)(2,1)S(1)} %get-tuple-element.137), channel_id=1, source_target_pairs={{0,24},{8,16},{16,8},{24,0},{1,25},{9,17},{17,9},{25,1},{2,26},{10... | collective-permute-start | bytes 4718600 | tf_op jit(solution)/shard_map/ppermute | solution.py:469
  54.7 3.3 %hidden_part.6 = (bf16[256,384]{1,0:T(8,128)(2,1)S(1)}, bf16[256,384]{1,0:T(8,128)(2,1)S(1)}, bf16[256,384]{1,0:T(8,128)(2,1)S(1)}, bf16[1024,768]{1,0:T(8,128)(2,1)S(1)}, bf16[1024,768]{1,0:T(8,128)(2,1)S(1)}) custom-call(s32[4]{0:T(128)S(1)} %pad_add_fusion.coords, bf16[384,2048]{1,0:T(8,128)(2,1)S(1)} %get-tuple-element.78.hid, ...), custom_call_target="tpu_custom_call" | custom-call | tf_op jit(solution)/shard_map/hidden_part/pallas_call | solution.py:318
  58.6 3.3 %hidden_part.5 = (bf16[256,384]{1,0:T(8,128)(2,1)S(1)}, bf16[256,384]{1,0:T(8,128)(2,1)S(1)}, bf16[256,384]{1,0:T(8,128)(2,1)S(1)}, bf16[1024,768]{1,0:T(8,128)(2,1)S(1)}, bf16[1024,768]{1,0:T(8,128)(2,1)S(1)}) custom-call(s32[4]{0:T(128)S(1)} %pad_add_fusion.coords, bf16[384,2048]{1,0:T(8,128)(2,1)S(1)} %get-tuple-element.78.hid, ...), custom_call_target="tpu_custom_call" | custom-call | tf_op jit(solution)/shard_map/hidden_part/pallas_call | solution.py:318
  61.9 2.8 %collective-permute-start.26 = (bf16[1024,768]{1,0:T(8,128)(2,1)S(1)}, bf16[1024,768]{1,0:T(8,128)(2,1)S(1)}, u32[]{:S(2)}, u32[]{:S(2)}) collective-permute-start(bf16[1024,768]{1,0:T(8,128)(2,1)S(1)} %get-tuple-element.121), channel_id=1, source_target_pairs={{0,96},{32,64},{64,32},{96,0},{1,97},{33,65},{65,33},{97,1},{2,98}... | collective-permute-start | bytes 4718600 | tf_op jit(solution)/shard_map/ppermute | solution.py:469
  64.7 3.3 %hidden_part.4 = (bf16[256,384]{1,0:T(8,128)(2,1)S(1)}, bf16[256,384]{1,0:T(8,128)(2,1)S(1)}, bf16[256,384]{1,0:T(8,128)(2,1)S(1)}, bf16[1024,768]{1,0:T(8,128)(2,1)S(1)}, bf16[1024,768]{1,0:T(8,128)(2,1)S(1)}) custom-call(s32[4]{0:T(128)S(1)} %pad_add_fusion.coords, bf16[384,2048]{1,0:T(8,128)(2,1)S(1)} %get-tuple-element.78.hid, ...), custom_call_target="tpu_custom_call" | custom-call | tf_op jit(solution)/shard_map/hidden_part/pallas_call | solution.py:318
  68.4 5.0 %back.3 = (bf16[4,256,384]{2,1,0:T(8,128)(2,1)S(1)}, bf16[4,256,384]{2,1,0:T(8,128)(2,1)S(1)}) custom-call(s32[4]{0:T(128)S(1)} %pad_add_fusion.coords, bf16[256,384]{1,0:T(8,128)(2,1)S(1)} %get-tuple-element.93.refs_0_, bf16[256,384]{1,0:T(8,128)(2,1)S(1)} %get-tuple-element.94.refs_1_, bf16[256,384]{1,0:T(8,128)(2,1)S(1)} %get-tuple-element.95.refs_2_, ...), custom_call_target="tpu_custom_call" | custom-call | tf_op jit(solution)/shard_map/back/pallas_call | solution.py:367
  73.5 2.9 %back.2 = (bf16[4,256,384]{2,1,0:T(8,128)(2,1)S(1)}, bf16[4,256,384]{2,1,0:T(8,128)(2,1)S(1)}) custom-call(s32[4]{0:T(128)S(1)} %pad_add_fusion.coords, bf16[256,384]{1,0:T(8,128)(2,1)S(1)} %get-tuple-element.82.refs_0_, bf16[256,384]{1,0:T(8,128)(2,1)S(1)} %get-tuple-element.83.refs_1_, bf16[256,384]{1,0:T(8,128)(2,1)S(1)} %get-tuple-element.84.refs_2_, ...), custom_call_target="tpu_custom_call" | custom-call | tf_op jit(solution)/shard_map/back/pallas_call | solution.py:367
  76.4 13.6 %collective-permute-done.34.came = bf16[1024,768]{1,0:T(8,128)(2,1)S(1)} collective-permute-done((bf16[1024,768]{1,0:T(8,128)(2,1)S(1)}, bf16[1024,768]{1,0:T(8,128)(2,1)S(1)}, u32[]{:S(2)}, u32[]{:S(2)}) %collective-permute-start.34) | collective-permute-done | bytes 1572896 | tf_op jit(solution)/shard_map/ppermute | solution.py:469
  90.3 4.5 %collective-permute-done.30.came = bf16[1024,768]{1,0:T(8,128)(2,1)S(1)} collective-permute-done((bf16[1024,768]{1,0:T(8,128)(2,1)S(1)}, bf16[1024,768]{1,0:T(8,128)(2,1)S(1)}, u32[]{:S(2)}, u32[]{:S(2)}) %collective-permute-start.30) | collective-permute-done | bytes 1572896 | tf_op jit(solution)/shard_map/ppermute | solution.py:469
  95.5 4.0 %collective-permute-done.26.came = bf16[1024,768]{1,0:T(8,128)(2,1)S(1)} collective-permute-done((bf16[1024,768]{1,0:T(8,128)(2,1)S(1)}, bf16[1024,768]{1,0:T(8,128)(2,1)S(1)}, u32[]{:S(2)}, u32[]{:S(2)}) %collective-permute-start.26) | collective-permute-done | bytes 1572896 | tf_op jit(solution)/shard_map/ppermute | solution.py:469
  101.0 3.1 %collective-permute-done.22.came = bf16[1024,768]{1,0:T(8,128)(2,1)S(1)} collective-permute-done((bf16[1024,768]{1,0:T(8,128)(2,1)S(1)}, bf16[1024,768]{1,0:T(8,128)(2,1)S(1)}, u32[]{:S(2)}, u32[]{:S(2)}) %collective-permute-start.22) | collective-permute-done | bytes 1572896 | tf_op jit(solution)/shard_map/ppermute | solution.py:469
  108.1 5.5 %collective-permute-done.35.came = bf16[512,768]{1,0:T(8,128)(2,1)S(1)} collective-permute-done((bf16[512,768]{1,0:T(8,128)(2,1)S(1)}, bf16[512,768]{1,0:T(8,128)(2,1)S(1)}, u32[]{:S(2)}, u32[]{:S(2)}) %collective-permute-start.35) | collective-permute-done | bytes 786464 | tf_op jit(solution)/shard_map/ppermute | solution.py:469
  114.5 4.8 %collective-permute-done.31.came = bf16[512,768]{1,0:T(8,128)(2,1)S(1)} collective-permute-done((bf16[512,768]{1,0:T(8,128)(2,1)S(1)}, bf16[512,768]{1,0:T(8,128)(2,1)S(1)}, u32[]{:S(2)}, u32[]{:S(2)}) %collective-permute-start.31) | collective-permute-done | bytes 786464 | tf_op jit(solution)/shard_map/ppermute | solution.py:469
  119.3 2.7 %collective-permute-start.36 = (bf16[256,768]{1,0:T(8,128)(2,1)S(1)}, bf16[256,768]{1,0:T(8,128)(2,1)S(1)}, u32[]{:S(2)}, u32[]{:S(2)}) collective-permute-start(bf16[256,768]{1,0:T(8,128)(2,1)S(1)} %get-tuple-element.141), channel_id=1, source_target_pairs={{0,96},{32,64},{64,32},{96,0},{1,97},{33,65},{65,33},{97,1},{2,98}... | collective-permute-start | bytes 1179656 | tf_op jit(solution)/shard_map/ppermute | solution.py:469
  123.7 3.0 %collective-permute-done.23.came = bf16[512,768]{1,0:T(8,128)(2,1)S(1)} collective-permute-done((bf16[512,768]{1,0:T(8,128)(2,1)S(1)}, bf16[512,768]{1,0:T(8,128)(2,1)S(1)}, u32[]{:S(2)}, u32[]{:S(2)}) %collective-permute-start.23) | collective-permute-done | bytes 786464 | tf_op jit(solution)/shard_map/ppermute | solution.py:469
  129.3 3.0 %collective-permute-start.21 = (bf16[256,384]{1,0:T(8,128)(2,1)S(1)}, bf16[256,384]{1,0:T(8,128)(2,1)S(1)}, u32[]{:S(2)}, u32[]{:S(2)}) collective-permute-start(bf16[256,384]{1,0:T(8,128)(2,1)S(1)} %get-tuple-element.106), channel_id=1, source_target_pairs={{0,4},{2,6},{4,0},{6,2},{1,5},{3,7},{5,1},{7,3},{8,12},{10,14},{12... | collective-permute-start | bytes 589832 | tf_op jit(solution)/shard_map/ppermute | solution.py:397
  133.7 4.8 %collective-permute-done.21.refs_2_ = bf16[256,384]{1,0:T(8,128)(2,1)S(1)} collective-permute-done((bf16[256,384]{1,0:T(8,128)(2,1)S(1)}, bf16[256,384]{1,0:T(8,128)(2,1)S(1)}, u32[]{:S(2)}, u32[]{:S(2)}) %collective-permute-start.21) | collective-permute-done | bytes 196640 | tf_op jit(solution)/shard_map/ppermute | solution.py:397
  142.9 4.3 %all-to-all-start.1 = ((bf16[16,48,256]{2,1,0:T(8,128)(2,1)}), bf16[16,48,256]{2,1,0:T(8,128)(2,1)S(1)}, u32[]{:S(2)}, u32[]{:S(2)}) async-start(bf16[16,48,256]{2,1,0:T(8,128)(2,1)} %copy-done.8), calls=%async_computation.1 | async-start | bytes 786432 | tf_op jit(solution)/shard_map/all_to_all | solution.py:51
  147.9 4.0 %collective-permute-start.17 = (bf16[256,384]{1,0:T(8,128)(2,1)}, bf16[256,384]{1,0:T(8,128)(2,1)S(1)}, u32[]{:S(2)}, u32[]{:S(2)}) collective-permute-start(bf16[256,384]{1,0:T(8,128)(2,1)} %copy-done.27), channel_id=1, source_target_pairs={{0,4},{2,6},{4,0},{6,2},{1,5},{3,7},{5,1},{7,3},{8,12},{10,14},{12... | collective-permute-start | bytes 589832 | tf_op jit(solution)/shard_map/ppermute | solution.py:397
  156.0 2.1 %collective-permute-start.33 = (bf16[128,768]{1,0:T(8,128)(2,1)}, bf16[128,768]{1,0:T(8,128)(2,1)S(1)}, u32[]{:S(2)}, u32[]{:S(2)}) collective-permute-start(bf16[128,768]{1,0:T(8,128)(2,1)} %get-tuple-element.135), channel_id=1, source_target_pairs={{0,96},{32,64},{64,32},{96,0},{1,97},{33,65},{65,33},{97,1},{2,98}... | collective-permute-start | bytes 589832 | tf_op jit(solution)/shard_map/ppermute | solution.py:469
  160.8 2.1 %collective-permute-start.25 = (bf16[128,768]{1,0:T(8,128)(2,1)S(1)}, bf16[128,768]{1,0:T(8,128)(2,1)S(1)}, u32[]{:S(2)}, u32[]{:S(2)}) collective-permute-start(bf16[128,768]{1,0:T(8,128)(2,1)S(1)} %get-tuple-element.119), channel_id=1, source_target_pairs={{0,24},{8,16},{16,8},{24,0},{1,25},{9,17},{17,9},{25,1},{2,26},{10... | collective-permute-start | bytes 589832 | tf_op jit(solution)/shard_map/ppermute | solution.py:469
  (134 shorter events, 46.6 us)
Async XLA Ops:
  3.7 18.0 %all-to-all-start = ((bf16[16,48,256]{2,1,0:T(8,128)(2,1)}), bf16[16,48,256]{2,1,0:T(8,128)(2,1)S(1)}, u32[]{:S(2)}, u32[]{:S(2)}) async-start(bf16[16,48,256]{2,1,0:T(8,128)(2,1)} %stats.1), calls=%async_computation | async-start | bytes 786432 | tf_op jit(solution)/shard_map/all_to_all | solution.py:51
  12.1 9.5 %collective-permute-start.8 = (bf16[384,256]{1,0:T(8,128)(2,1)}, bf16[384,256]{1,0:T(8,128)(2,1)S(1)}, u32[]{:S(2)}, u32[]{:S(2)}) collective-permute-start(bf16[384,256]{1,0:T(8,128)(2,1)} %cotangent.1), channel_id=1, source_target_pairs={{0,4},{2,6},{4,0},{6,2},{1,5},{3,7},{5,1},{7,3},{8,12},{10,14},{12... | collective-permute-start | bytes 589832 | tf_op jit(solution)/shard_map/ppermute | solution.py:65
  15.0 13.1 %collective-permute-start.9 = (bf16[384,256]{1,0:T(8,128)(2,1)}, bf16[384,256]{1,0:T(8,128)(2,1)S(1)}, u32[]{:S(2)}, u32[]{:S(2)}) collective-permute-start(bf16[384,256]{1,0:T(8,128)(2,1)} %cotangent.1), channel_id=1, source_target_pairs={{0,2},{2,4},{4,6},{6,0},{1,3},{3,5},{5,7},{7,1},{8,10},{10,12},{12... | collective-permute-start | bytes 589832 | tf_op jit(solution)/shard_map/ppermute | solution.py:65
  15.0 16.7 %collective-permute-start.10 = (bf16[384,256]{1,0:T(8,128)(2,1)}, bf16[384,256]{1,0:T(8,128)(2,1)S(1)}, u32[]{:S(2)}, u32[]{:S(2)}) collective-permute-start(bf16[384,256]{1,0:T(8,128)(2,1)} %cotangent.1), channel_id=1, source_target_pairs={{0,1},{1,0},{2,3},{3,2},{4,5},{5,4},{6,7},{7,6},{8,9},{9,8},{10,11... | collective-permute-start | bytes 589832 | tf_op jit(solution)/shard_map/ppermute | solution.py:69
  19.6 12.0 %collective-permute-start.11 = (bf16[384,256]{1,0:T(8,128)(2,1)S(1)}, bf16[384,256]{1,0:T(8,128)(2,1)S(1)}, u32[]{:S(2)}, u32[]{:S(2)}) collective-permute-start(bf16[384,256]{1,0:T(8,128)(2,1)S(1)} %collective-permute-done.7.refs_1_), channel_id=1, source_target_pairs={{0,1},{1,0},{2,3},{3,2},{4,5},{5,4},{6,7},{7,6},{8,9},{9,8},{10,11... | collective-permute-start | bytes 589832 | tf_op jit(solution)/shard_map/ppermute | solution.py:69
  21.6 10.2 %collective-permute-start.12 = (bf16[384,256]{1,0:T(8,128)(2,1)S(1)}, bf16[384,256]{1,0:T(8,128)(2,1)S(1)}, u32[]{:S(2)}, u32[]{:S(2)}) collective-permute-start(bf16[384,256]{1,0:T(8,128)(2,1)S(1)} %collective-permute-done.8.refs_2_), channel_id=1, source_target_pairs={{0,1},{1,0},{2,3},{3,2},{4,5},{5,4},{6,7},{7,6},{8,9},{9,8},{10,11... | collective-permute-start | bytes 589832 | tf_op jit(solution)/shard_map/ppermute | solution.py:69
  25.8 9.5 %collective-permute-start = (bf16[384,256]{1,0:T(8,128)(2,1)S(1)}, bf16[384,256]{1,0:T(8,128)(2,1)S(1)}, u32[]{:S(2)}, u32[]{:S(2)}) collective-permute-start(bf16[384,256]{1,0:T(8,128)(2,1)S(1)} %get-tuple-element.77.refs_0_), channel_id=1, source_target_pairs={{0,6},{2,0},{4,2},{6,4},{1,7},{3,1},{5,3},{7,5},{8,14},{10,8},{12,... | collective-permute-start | bytes 589832 | tf_op jit(solution)/shard_map/ppermute | solution.py:65
  31.8 15.5 %collective-permute-start.3 = (bf16[384,256]{1,0:T(8,128)(2,1)S(1)}, bf16[384,256]{1,0:T(8,128)(2,1)S(1)}, u32[]{:S(2)}, u32[]{:S(2)}) collective-permute-start(bf16[384,256]{1,0:T(8,128)(2,1)S(1)} %get-tuple-element.77.refs_0_), channel_id=1, source_target_pairs={{0,1},{1,0},{2,3},{3,2},{4,5},{5,4},{6,7},{7,6},{8,9},{9,8},{10,11... | collective-permute-start | bytes 589832 | tf_op jit(solution)/shard_map/ppermute | solution.py:69
  35.3 11.9 %collective-permute-start.4 = (bf16[384,256]{1,0:T(8,128)(2,1)S(1)}, bf16[384,256]{1,0:T(8,128)(2,1)S(1)}, u32[]{:S(2)}, u32[]{:S(2)}) collective-permute-start(bf16[384,256]{1,0:T(8,128)(2,1)S(1)} %collective-permute-done.refs_1_), channel_id=1, source_target_pairs={{0,1},{1,0},{2,3},{3,2},{4,5},{5,4},{6,7},{7,6},{8,9},{9,8},{10,11... | collective-permute-start | bytes 589832 | tf_op jit(solution)/shard_map/ppermute | solution.py:69
  37.4 9.8 %collective-permute-start.5 = (bf16[384,256]{1,0:T(8,128)(2,1)S(1)}, bf16[384,256]{1,0:T(8,128)(2,1)S(1)}, u32[]{:S(2)}, u32[]{:S(2)}) collective-permute-start(bf16[384,256]{1,0:T(8,128)(2,1)S(1)} %collective-permute-done.1.refs_2_), channel_id=1, source_target_pairs={{0,1},{1,0},{2,3},{3,2},{4,5},{5,4},{6,7},{7,6},{8,9},{9,8},{10,11... | collective-permute-start | bytes 589832 | tf_op jit(solution)/shard_map/ppermute | solution.py:69
  51.9 38.1 %collective-permute-start.34 = (bf16[1024,768]{1,0:T(8,128)(2,1)S(1)}, bf16[1024,768]{1,0:T(8,128)(2,1)S(1)}, u32[]{:S(2)}, u32[]{:S(2)}) collective-permute-start(bf16[1024,768]{1,0:T(8,128)(2,1)S(1)} %get-tuple-element.137), channel_id=1, source_target_pairs={{0,24},{8,16},{16,8},{24,0},{1,25},{9,17},{17,9},{25,1},{2,26},{10... | collective-permute-start | bytes 4718600 | tf_op jit(solution)/shard_map/ppermute | solution.py:469
  58.1 36.8 %collective-permute-start.30 = (bf16[1024,768]{1,0:T(8,128)(2,1)S(1)}, bf16[1024,768]{1,0:T(8,128)(2,1)S(1)}, u32[]{:S(2)}, u32[]{:S(2)}) collective-permute-start(bf16[1024,768]{1,0:T(8,128)(2,1)S(1)} %get-tuple-element.129), channel_id=1, source_target_pairs={{0,8},{8,0},{16,24},{24,16},{1,9},{9,1},{17,25},{25,17},{2,10},{10... | collective-permute-start | bytes 4718600 | tf_op jit(solution)/shard_map/ppermute | solution.py:469
  61.9 37.6 %collective-permute-start.26 = (bf16[1024,768]{1,0:T(8,128)(2,1)S(1)}, bf16[1024,768]{1,0:T(8,128)(2,1)S(1)}, u32[]{:S(2)}, u32[]{:S(2)}) collective-permute-start(bf16[1024,768]{1,0:T(8,128)(2,1)S(1)} %get-tuple-element.121), channel_id=1, source_target_pairs={{0,96},{32,64},{64,32},{96,0},{1,97},{33,65},{65,33},{97,1},{2,98}... | collective-permute-start | bytes 4718600 | tf_op jit(solution)/shard_map/ppermute | solution.py:469
  68.0 36.1 %collective-permute-start.22 = (bf16[1024,768]{1,0:T(8,128)(2,1)S(1)}, bf16[1024,768]{1,0:T(8,128)(2,1)S(1)}, u32[]{:S(2)}, u32[]{:S(2)}) collective-permute-start(bf16[1024,768]{1,0:T(8,128)(2,1)S(1)} %get-tuple-element.113), channel_id=1, source_target_pairs={{0,32},{32,0},{64,96},{96,64},{1,33},{33,1},{65,97},{97,65},{2,34}... | collective-permute-start | bytes 4718600 | tf_op jit(solution)/shard_map/ppermute | solution.py:469
  73.4 31.4 %collective-permute-start.18 = (bf16[4,256,384]{2,1,0:T(8,128)(2,1)S(1)}, bf16[4,256,384]{2,1,0:T(8,128)(2,1)S(1)}, u32[]{:S(2)}, u32[]{:S(2)}) collective-permute-start(bf16[4,256,384]{2,1,0:T(8,128)(2,1)S(1)} %get-tuple-element.102), channel_id=1, source_target_pairs={{0,1},{1,0},{2,3},{3,2},{4,5},{5,4},{6,7},{7,6},{8,9},{9,8},{10,11... | collective-permute-start | bytes 2359304 | tf_op jit(solution)/shard_map/ppermute | solution.py:384
  89.9 16.4 %collective-permute-start.14 = (bf16[4,256,384]{2,1,0:T(8,128)(2,1)S(1)}, bf16[4,256,384]{2,1,0:T(8,128)(2,1)S(1)}, u32[]{:S(2)}, u32[]{:S(2)}) collective-permute-start(bf16[4,256,384]{2,1,0:T(8,128)(2,1)S(1)} %get-tuple-element.87), channel_id=1, source_target_pairs={{0,1},{1,0},{2,3},{3,2},{4,5},{5,4},{6,7},{7,6},{8,9},{9,8},{10,11... | collective-permute-start | bytes 2359304 | tf_op jit(solution)/shard_map/ppermute | solution.py:384
  94.8 18.8 %collective-permute-start.35 = (bf16[512,768]{1,0:T(8,128)(2,1)S(1)}, bf16[512,768]{1,0:T(8,128)(2,1)S(1)}, u32[]{:S(2)}, u32[]{:S(2)}) collective-permute-start(bf16[512,768]{1,0:T(8,128)(2,1)S(1)} %get-tuple-element.139), channel_id=1, source_target_pairs={{0,8},{8,0},{16,24},{24,16},{1,9},{9,1},{17,25},{25,17},{2,10},{10... | collective-permute-start | bytes 2359304 | tf_op jit(solution)/shard_map/ppermute | solution.py:469
  99.5 19.8 %collective-permute-start.31 = (bf16[512,768]{1,0:T(8,128)(2,1)S(1)}, bf16[512,768]{1,0:T(8,128)(2,1)S(1)}, u32[]{:S(2)}, u32[]{:S(2)}) collective-permute-start(bf16[512,768]{1,0:T(8,128)(2,1)S(1)} %get-tuple-element.131), channel_id=1, source_target_pairs={{0,24},{8,16},{16,8},{24,0},{1,25},{9,17},{17,9},{25,1},{2,26},{10... | collective-permute-start | bytes 2359304 | tf_op jit(solution)/shard_map/ppermute | solution.py:469
  104.1 18.7 %collective-permute-start.27 = (bf16[512,768]{1,0:T(8,128)(2,1)S(1)}, bf16[512,768]{1,0:T(8,128)(2,1)S(1)}, u32[]{:S(2)}, u32[]{:S(2)}) collective-permute-start(bf16[512,768]{1,0:T(8,128)(2,1)S(1)} %get-tuple-element.123), channel_id=1, source_target_pairs={{0,32},{32,0},{64,96},{96,64},{1,33},{33,1},{65,97},{97,65},{2,34}... | collective-permute-start | bytes 2359304 | tf_op jit(solution)/shard_map/ppermute | solution.py:469
  104.8 21.9 %collective-permute-start.23 = (bf16[512,768]{1,0:T(8,128)(2,1)S(1)}, bf16[512,768]{1,0:T(8,128)(2,1)S(1)}, u32[]{:S(2)}, u32[]{:S(2)}) collective-permute-start(bf16[512,768]{1,0:T(8,128)(2,1)S(1)} %get-tuple-element.115), channel_id=1, source_target_pairs={{0,96},{32,64},{64,32},{96,0},{1,97},{33,65},{65,33},{97,1},{2,98}... | collective-permute-start | bytes 2359304 | tf_op jit(solution)/shard_map/ppermute | solution.py:469
  106.4 22.3 %collective-permute-start.19 = (bf16[256,384]{1,0:T(8,128)(2,1)S(1)}, bf16[256,384]{1,0:T(8,128)(2,1)S(1)}, u32[]{:S(2)}, u32[]{:S(2)}) collective-permute-start(bf16[256,384]{1,0:T(8,128)(2,1)S(1)} %get-tuple-element.104), channel_id=1, source_target_pairs={{0,2},{2,4},{4,6},{6,0},{1,3},{3,5},{5,7},{7,1},{8,10},{10,12},{12... | collective-permute-start | bytes 589832 | tf_op jit(solution)/shard_map/ppermute | solution.py:397
  113.7 15.6 %collective-permute-start.20 = (bf16[256,384]{1,0:T(8,128)(2,1)S(1)}, bf16[256,384]{1,0:T(8,128)(2,1)S(1)}, u32[]{:S(2)}, u32[]{:S(2)}) collective-permute-start(bf16[256,384]{1,0:T(8,128)(2,1)S(1)} %get-tuple-element.105), channel_id=1, source_target_pairs={{0,6},{2,0},{4,2},{6,4},{1,7},{3,1},{5,3},{7,5},{8,14},{10,8},{12,... | collective-permute-start | bytes 589832 | tf_op jit(solution)/shard_map/ppermute | solution.py:397
  119.3 20.1 %collective-permute-start.36 = (bf16[256,768]{1,0:T(8,128)(2,1)S(1)}, bf16[256,768]{1,0:T(8,128)(2,1)S(1)}, u32[]{:S(2)}, u32[]{:S(2)}) collective-permute-start(bf16[256,768]{1,0:T(8,128)(2,1)S(1)} %get-tuple-element.141), channel_id=1, source_target_pairs={{0,96},{32,64},{64,32},{96,0},{1,97},{33,65},{65,33},{97,1},{2,98}... | collective-permute-start | bytes 1179656 | tf_op jit(solution)/shard_map/ppermute | solution.py:469
  122.8 25.1 %collective-permute-start.32 = (bf16[256,768]{1,0:T(8,128)(2,1)}, bf16[256,768]{1,0:T(8,128)(2,1)S(1)}, u32[]{:S(2)}, u32[]{:S(2)}) collective-permute-start(bf16[256,768]{1,0:T(8,128)(2,1)} %get-tuple-element.133), channel_id=1, source_target_pairs={{0,32},{32,0},{64,96},{96,64},{1,33},{33,1},{65,97},{97,65},{2,34}... | collective-permute-start | bytes 1179656 | tf_op jit(solution)/shard_map/ppermute | solution.py:469
  126.7 25.9 %collective-permute-start.28 = (bf16[256,768]{1,0:T(8,128)(2,1)}, bf16[256,768]{1,0:T(8,128)(2,1)S(1)}, u32[]{:S(2)}, u32[]{:S(2)}) collective-permute-start(bf16[256,768]{1,0:T(8,128)(2,1)} %get-tuple-element.125), channel_id=1, source_target_pairs={{0,24},{8,16},{16,8},{24,0},{1,25},{9,17},{17,9},{25,1},{2,26},{10... | collective-permute-start | bytes 1179656 | tf_op jit(solution)/shard_map/ppermute | solution.py:469
  128.7 27.4 %collective-permute-start.24 = (bf16[256,768]{1,0:T(8,128)(2,1)}, bf16[256,768]{1,0:T(8,128)(2,1)}, u32[]{:S(2)}, u32[]{:S(2)}) collective-permute-start(bf16[256,768]{1,0:T(8,128)(2,1)} %get-tuple-element.117), channel_id=1, source_target_pairs={{0,8},{8,0},{16,24},{24,16},{1,9},{9,1},{17,25},{25,17},{2,10},{10... | collective-permute-start | bytes 1179656 | tf_op jit(solution)/shard_map/ppermute | solution.py:469
  138.5 20.7 %collective-permute-start.15 = (bf16[256,384]{1,0:T(8,128)(2,1)}, bf16[256,384]{1,0:T(8,128)(2,1)}, u32[]{:S(2)}, u32[]{:S(2)}) collective-permute-start(bf16[256,384]{1,0:T(8,128)(2,1)} %get-tuple-element.89), channel_id=1, source_target_pairs={{0,2},{2,4},{4,6},{6,0},{1,3},{3,5},{5,7},{7,1},{8,10},{10,12},{12... | collective-permute-start | bytes 589832 | tf_op jit(solution)/shard_map/ppermute | solution.py:397
  139.4 21.4 %collective-permute-start.16 = (bf16[256,384]{1,0:T(8,128)(2,1)}, bf16[256,384]{1,0:T(8,128)(2,1)}, u32[]{:S(2)}, u32[]{:S(2)}) collective-permute-start(bf16[256,384]{1,0:T(8,128)(2,1)} %get-tuple-element.90), channel_id=1, source_target_pairs={{0,6},{2,0},{4,2},{6,4},{1,7},{3,1},{5,3},{7,5},{8,14},{10,8},{12,... | collective-permute-start | bytes 589832 | tf_op jit(solution)/shard_map/ppermute | solution.py:397
  142.9 21.9 %all-to-all-start.1 = ((bf16[16,48,256]{2,1,0:T(8,128)(2,1)}), bf16[16,48,256]{2,1,0:T(8,128)(2,1)S(1)}, u32[]{:S(2)}, u32[]{:S(2)}) async-start(bf16[16,48,256]{2,1,0:T(8,128)(2,1)} %copy-done.8), calls=%async_computation.1 | async-start | bytes 786432 | tf_op jit(solution)/shard_map/all_to_all | solution.py:51
  147.9 15.0 %collective-permute-start.17 = (bf16[256,384]{1,0:T(8,128)(2,1)}, bf16[256,384]{1,0:T(8,128)(2,1)S(1)}, u32[]{:S(2)}, u32[]{:S(2)}) collective-permute-start(bf16[256,384]{1,0:T(8,128)(2,1)} %copy-done.27), channel_id=1, source_target_pairs={{0,4},{2,6},{4,0},{6,2},{1,5},{3,7},{5,1},{7,3},{8,12},{10,14},{12... | collective-permute-start | bytes 589832 | tf_op jit(solution)/shard_map/ppermute | solution.py:397
  152.6 13.6 %collective-permute-start.37 = (bf16[128,768]{1,0:T(8,128)(2,1)}, bf16[128,768]{1,0:T(8,128)(2,1)S(1)}, u32[]{:S(2)}, u32[]{:S(2)}) collective-permute-start(bf16[128,768]{1,0:T(8,128)(2,1)} %get-tuple-element.143), channel_id=1, source_target_pairs={{0,32},{32,0},{64,96},{96,64},{1,33},{33,1},{65,97},{97,65},{2,34}... | collective-permute-start | bytes 589832 | tf_op jit(solution)/shard_map/ppermute | solution.py:469
  156.0 10.2 %collective-permute-start.33 = (bf16[128,768]{1,0:T(8,128)(2,1)}, bf16[128,768]{1,0:T(8,128)(2,1)S(1)}, u32[]{:S(2)}, u32[]{:S(2)}) collective-permute-start(bf16[128,768]{1,0:T(8,128)(2,1)} %get-tuple-element.135), channel_id=1, source_target_pairs={{0,96},{32,64},{64,32},{96,0},{1,97},{33,65},{65,33},{97,1},{2,98}... | collective-permute-start | bytes 589832 | tf_op jit(solution)/shard_map/ppermute | solution.py:469
  (36 other events, 364.0 us)

commit v2 on v1

v2 whole, which is shorter than its diff:
```python
import jax
import jax.numpy as jnp
from jax import lax
from jax.experimental import pallas as pl
from jax.experimental.pallas import tpu as pltpu
from jax.sharding import Mesh
from jax.sharding import PartitionSpec as P


GHOST = 128
BLK = 16
RING = 4
NEAR = [(i, i ^ 1) for i in range(RING)]
FAR = [(i, RING - 1 - i) for i in range(RING)]
CORES = [(0, 1), (1, 0)]
EPSILON = 1e-05
MOMENTUM = 0.1


bf16 = jnp.bfloat16
f32 = jnp.float32


PATTERNS = (("z", 0), ("z", 1), ("x", 0), ("x", 1))
LENT = 128


def halving(i, first):
    near, far = i ^ 1, RING - 1 - i
    p, q = (near, far) if first == 0 else (far, near)
    return [RING - 1 - p if first == 0 else p ^ 1, p, q, i]


def row_blocks(coords, pattern):
    major, first = pattern
    hz, hx = halving(coords[0], first), halving(coords[1], first)
    if major == "z":
        return [RING * a + b for a in hz for b in hx]
    return [RING * a + b for b in hx for a in hz]


def feature_blocks(coords, other):
    core = coords[3] if other == 0 else 1 - coords[3]
    return [2 * ((coords[2] + k) & (RING - 1)) + core for k in range(RING)]


def shift(k):
    return [(i, (i + k) % RING) for i in range(RING)]


def vmem_spec():
    return pl.BlockSpec(memory_space=pltpu.VMEM)


def smem_spec():
    return pl.BlockSpec(memory_space=pltpu.SMEM)


def in_hbm(x):
    return pltpu.with_memory_space_constraint(x, pltpu.HBM)


def gathered(x):
    near = [x]
    for k in (1, 3, 2):
        near.append(lax.ppermute(x, "y", shift(-k)))
    near = [near[0], near[1], near[3], near[2]]
    far = []
    for k in range(RING):
        far.append(lax.ppermute(near[k], "c", CORES))
    return near + far


def block_sum(value):
    return jnp.sum(value, axis=0, keepdims=True)


def own_gain(coords, gain, feat):
    return gain[:, pl.ds(pl.multiple_of((2 * coords[2] + coords[3]) * feat, feat), feat)]


def add_kernel(left, right, out):
    out[...] = left[...] + right[...]


def pair_added(left, right):
    return pl.pallas_call(
        add_kernel,
        out_shape=jax.ShapeDtypeStruct(left.shape, left.dtype),
        in_specs=[vmem_spec()] * 2,
        out_specs=vmem_spec(),
        compiler_params=limits(1),
        name="pair_added",
    )(left, right)


def tok_halves(x):
    for i, (axis, pairs) in enumerate((("z", NEAR), ("z", FAR), ("x", NEAR), ("x", FAR)), 1):
        came = lax.ppermute(x, axis, pairs)
        if i < 4:
            x = pair_added(x, came)
    return x, came


def ring_sum_kernel(*refs):
    ins, out = refs[:-1], refs[-1]
    out[...] = (ins[0][...] + ins[3][...]) + (ins[1][...] + ins[2][...])


def ring_pieces(x, axis):
    came = [x]
    for k in (1, 3, 2):
        came.append(lax.ppermute(x, axis, shift(k)))
    return came


def ring_sum(x, axis):
    pieces = ring_pieces(x, axis)
    return pl.pallas_call(
        ring_sum_kernel,
        out_shape=jax.ShapeDtypeStruct(x.shape, x.dtype),
        in_specs=[vmem_spec()] * RING,
        out_specs=vmem_spec(),
        compiler_params=limits(1),
        name="ring_sum",
    )(*pieces)


STAGE_CUTS = 4


def stage_kernel(*refs):
    count = (len(refs) - 1) // 2
    sems = refs[-1]
    copies = []
    for i in range(count):
        source, out = refs[i], refs[count + i]
        rows = source.shape[0] // STAGE_CUTS
        for j in range(STAGE_CUTS):
            part = pl.ds(j * rows, rows)
            copies.append(
                pltpu.make_async_copy(source.at[part], out.at[part], sems.at[i * STAGE_CUTS + j])
            )
    for copy in copies:
        copy.start()
    for copy in copies:
        copy.wait()


def staged(*weights):
    return pl.pallas_call(
        stage_kernel,
        out_shape=tuple(pltpu.VMEM(w.shape, w.dtype) for w in weights),
        in_specs=[pl.BlockSpec(memory_space=pltpu.HBM)] * len(weights),
        out_specs=(vmem_spec(),) * len(weights),
        scratch_shapes=[pltpu.SemaphoreType.DMA((STAGE_CUTS * len(weights),))],
        compiler_params=limits(1),
        name="staged",
    )(*[in_hbm(w) for w in weights])


def stats_kernel(groups, coords, tokens, cotangent, out, both):
    rows = tokens.shape[0]
    both[:rows, :] = tokens[...]
    both[rows:, :] = cotangent[...]
    out[...] = jnp.zeros_like(out)
    for b in range(rows // BLK):
        value = tokens[b * BLK : (b + 1) * BLK, :].astype(f32)
        row = pl.ds(groups[b], 1)
        out[row, :] = out[row, :] + block_sum(value * value)


def stats(groups, coords, tokens, cotangent, groups_total):
    rows, feat = tokens.shape
    return pl.pallas_call(
        stats_kernel,
        out_shape=(
            jax.ShapeDtypeStruct((groups_total, feat), f32),
            jax.ShapeDtypeStruct((2 * rows, feat), bf16),
        ),
        in_specs=[smem_spec(), smem_spec(), vmem_spec(), vmem_spec()],
        out_specs=(vmem_spec(),) * 2,
        compiler_params=limits(4),
        name="stats",
    )(in_hbm(groups), coords, in_hbm(tokens), in_hbm(cotangent))


def table_kernel(a, b, c, d, table, quad):
    quad_mean = ((a[...] + d[...]) + (b[...] + c[...])) * (1.0 / GHOST)
    quad[...] = quad_mean
    table[...] = lax.rsqrt(quad_mean + EPSILON)


def scale_table(pieces):
    out = jax.ShapeDtypeStruct(pieces[0].shape, f32)
    return pl.pallas_call(
        table_kernel,
        out_shape=(out, out),
        in_specs=[vmem_spec()] * RING,
        out_specs=(vmem_spec(),) * 2,
        compiler_params=limits(2),
        name="scale_table",
    )(*pieces)


def partial_kernel(groups, tokens, table, own, *refs):
    came, (grad, out) = refs[:-2], refs[-2:]
    total = own[...]
    for ref in came:
        total = total + ref[...].astype(f32)
    grad[...] = total.T
    out[...] = jnp.zeros_like(out)
    for b in range(tokens.shape[0] // BLK):
        rows = slice(b * BLK, (b + 1) * BLK)
        row = pl.ds(groups[b], 1)
        normed = tokens[rows, :].astype(f32) * table[row, :]
        out[row, :] = out[row, :] + block_sum(grad[rows, :] * normed)


def partials(groups, tokens, table, own, came):
    rows, feat = tokens.shape
    return pl.pallas_call(
        partial_kernel,
        out_shape=(
            jax.ShapeDtypeStruct((rows, feat), f32),
            jax.ShapeDtypeStruct(table.shape, f32),
        ),
        in_specs=[smem_spec()] + [vmem_spec()] * (3 + len(came)),
        out_specs=(vmem_spec(),) * 2,
        compiler_params=limits(6),
        name="partials",
    )(in_hbm(groups), tokens, table, own, *came)


def input_kernel(groups, coords, tokens, cotangent, gain, table, grad, mine, came, out, grad_gain, acc):
    partial = mine[...] + came[...]
    grad_gain[...] = jnp.sum(partial, axis=0, keepdims=True)
    gain_row = own_gain(coords, gain, tokens.shape[1])
    acc[...] = gain_row * partial * (1.0 / GHOST)
    for b in range(tokens.shape[0] // BLK):
        rows = slice(b * BLK, (b + 1) * BLK)
        row = pl.ds(groups[b], 1)
        scale = table[row, :]
        normed = tokens[rows, :].astype(f32) * scale
        inner = gain_row * grad[rows, :] - normed * acc[row, :]
        out[rows, :] = (cotangent[rows, :].astype(f32) + scale * inner).astype(bf16)


def input_grads(groups, coords, tokens, cotangent, gain, table, grad, mine, came):
    rows, feat = tokens.shape
    return pl.pallas_call(
        input_kernel,
        out_shape=(
            jax.ShapeDtypeStruct((rows, feat), bf16),
            jax.ShapeDtypeStruct((1, feat), f32),
        ),
        in_specs=[smem_spec(), smem_spec()] + [vmem_spec()] * 7,
        out_specs=(vmem_spec(),) * 2,
        scratch_shapes=[pltpu.VMEM(table.shape, f32)],
        compiler_params=limits(6),
        name="input_grads",
    )(in_hbm(groups), coords, tokens, cotangent, gain, table, grad, mine, came)


def branch_kernel(tokens, running, quad, own, *refs):
    came, (out, running_new) = refs[:-2], refs[-2:]
    total = own[...]
    for ref in came:
        total = total + ref[...].astype(f32)
    out[...] = (tokens[...].astype(f32) + total.T).astype(bf16)
    mean = jnp.sum(quad[...], axis=0, keepdims=True) / quad.shape[0]
    running_new[...] = (1.0 - MOMENTUM) * running[...] + MOMENTUM * mean


def branch_out(tokens, running, quad, own, came):
    return pl.pallas_call(
        branch_kernel,
        out_shape=(
            jax.ShapeDtypeStruct(tokens.shape, bf16),
            jax.ShapeDtypeStruct(running.shape, f32),
        ),
        in_specs=[vmem_spec()] * (4 + len(came)),
        out_specs=(vmem_spec(),) * 2,
        compiler_params=limits(6),
        name="branch_out",
    )(tokens, in_hbm(running), quad, own, *came)


def limits(mib):
    return pltpu.CompilerParams(vmem_limit_bytes=mib << 20)


def places(coords):
    return feature_blocks(coords, 0) + feature_blocks(coords, 1)


def cotangent_kernel(coords, *refs):
    pieces, (out, turned) = refs[:-2], refs[-2:]
    rows, width = out.shape[0], pieces[0].shape[1]
    for place, piece in zip(places(coords), pieces):
        first = pl.multiple_of(place * width, width)
        value = piece[rows:, :]
        out[:, pl.ds(first, width)] = value
        turned[pl.ds(first, width), :] = value.T


def normalize_kernel(groups, coords, gain, *refs):
    ins, (out, turned) = refs[:-2], refs[-2:]
    pieces, tables = ins[: len(ins) // 2], ins[len(ins) // 2 :]
    rows, width = out.shape[0], pieces[0].shape[1]
    for place, piece, table in zip(places(coords), pieces, tables):
        first = pl.multiple_of(place * width, width)
        gain_row = gain[:, pl.ds(first, width)]
        for b in range(rows // BLK):
            block = slice(b * BLK, (b + 1) * BLK)
            normed = piece[block, :].astype(f32) * table[pl.ds(groups[b], 1), :]
            out[block, pl.ds(first, width)] = (gain_row * normed).astype(bf16)
        turned[pl.ds(first, width), :] = out[:, pl.ds(first, width)].T


def assembled_shapes(pieces):
    rows, width = pieces[0].shape[0] // 2, pieces[0].shape[1] * len(pieces)
    return (jax.ShapeDtypeStruct((rows, width), bf16), jax.ShapeDtypeStruct((width, rows), bf16))


def cotangent_whole(coords, pieces):
    return pl.pallas_call(
        cotangent_kernel,
        out_shape=assembled_shapes(pieces),
        in_specs=[smem_spec()] + [vmem_spec()] * len(pieces),
        out_specs=(vmem_spec(), vmem_spec()),
        compiler_params=limits(12),
        name="cotangent_whole",
    )(coords, *pieces)


def normalized_whole(groups, coords, gain, pieces, tables):
    return pl.pallas_call(
        normalize_kernel,
        out_shape=assembled_shapes(pieces),
        in_specs=[smem_spec(), smem_spec()] + [vmem_spec()] * (1 + 2 * len(pieces)),
        out_specs=(vmem_spec(), vmem_spec()),
        compiler_params=limits(12),
        name="normalized_whole",
    )(in_hbm(groups), coords, gain, *pieces, *tables)


def rows_product(blocks, turned, right, send, keep, first):
    columns = slice(first, first + right.shape[1])
    half = len(blocks) // 2
    for part, out in ((blocks[:half], send), (blocks[half:], keep)):
        left = jnp.concatenate(
            [turned[pl.ds(pl.multiple_of(b * 128, 128), 128), :] for b in part], axis=0
        )
        out[:, columns] = jnp.dot(left, right, preferred_element_type=f32).astype(out.dtype)


def hidden_kernel(p, lent):
    def kernel(coords, hid, hid_t, dy, dy_t, gate_w, up_w, down_w, hidden_t, ggi_t, gl_t, *outs):
        gate = jnp.dot(hid[...], gate_w[...], preferred_element_type=f32)
        lift = jnp.dot(hid[...], up_w[...], preferred_element_type=f32)
        grad = jnp.dot(dy[...], down_w[...], preferred_element_type=f32)
        sigma = jax.nn.sigmoid(gate)
        act = gate * sigma
        hidden = (act * lift).astype(bf16)
        ggi = (grad * lift * sigma * (1.0 + gate * (1.0 - sigma))).astype(bf16)
        gl = (grad * act).astype(bf16)
        own = row_blocks(coords, PATTERNS[p])
        rows_product(own, dy_t, hidden[:, lent:], outs[0], outs[1], 0)
        both = jnp.concatenate([ggi, gl], axis=1)
        rows_product(own, hid_t, both, outs[0], outs[1], hidden.shape[1] - lent)
        if lent:
            rows_product(row_blocks(coords, PATTERNS[0]), dy_t, hidden[:, :lent], outs[2], outs[3], 0)
        hidden_t[...] = hidden.T
        ggi_t[...] = ggi.T
        gl_t[...] = gl.T

    return kernel


def hidden_part(p, coords, hid, hid_t, dy, dy_t, gate_w, up_w, down_w):
    rows, width = hid.shape
    part = gate_w.shape[1] // RING
    lent = LENT if p == RING - 1 else 0

    def fixed(*shape):
        return pl.BlockSpec(shape, lambda i: (0, 0))

    weight = pl.BlockSpec((width, part), lambda i: (0, p))
    halves = [3 * part - lent] * 2 + ([lent] * 2 if lent else [])
    shapes = [(part, rows)] * 3 + [(width // 2, n) for n in halves]
    return pl.pallas_call(
        hidden_kernel(p, lent),
        grid=(1,),
        out_shape=tuple(jax.ShapeDtypeStruct(shape, bf16) for shape in shapes),
        in_specs=[
            smem_spec(),
            fixed(rows, width),
            fixed(width, rows),
            fixed(rows, width),
            fixed(width, rows),
            weight,
            weight,
            weight,
        ],
        out_specs=tuple(fixed(*shape) for shape in shapes),
        compiler_params=limits(20),
        name="hidden_part",
    )(coords, hid, hid_t, dy, dy_t, gate_w, up_w, down_w)


def back_kernel(pairs):
    def kernel(coords, *refs):
        acts = refs[: pairs * RING]
        weights = refs[pairs * RING : pairs * RING + pairs]
        outs = refs[pairs * RING + pairs :]
        feat = outs[0].shape[1]
        for other, out in ((1, outs[0]), (0, outs[1])):
            total = None
            for j in range(pairs):
                act = jnp.concatenate([r[...] for r in acts[j * RING : (j + 1) * RING]], axis=0)
                left = jnp.concatenate(
                    [
                        weights[j][pl.ds(pl.multiple_of(b * feat, feat), feat), :]
                        for b in feature_blocks(coords, other)
                    ],
                    axis=0,
                )
                term = jnp.dot(left, act, preferred_element_type=f32)
                total = term if total is None else total + term
            for k in range(RING):
                out[k] = total[k * feat : (k + 1) * feat, :].astype(bf16)

    return kernel


def back(coords, acts, weights):
    rows = acts[0][0].shape[1]
    feat = weights[0].shape[0] // (2 * RING)
    pairs = len(weights)
    out = jax.ShapeDtypeStruct((RING, feat, rows), bf16)
    return pl.pallas_call(
        back_kernel(pairs),
        in_specs=[smem_spec()] + [vmem_spec()] * (pairs * RING + pairs),
        out_specs=(vmem_spec(), vmem_spec()),
        out_shape=(out, out),
        compiler_params=limits(20),
        name="back",
    )(coords, *[a for group in acts for a in group], *weights)


def chip_sum_kernel(near, other, own, *sends):
    own[...] = near[0].astype(f32) + other[0].astype(f32)
    for k, send in enumerate(sends, 1):
        send[...] = (near[k].astype(f32) + other[k].astype(f32)).astype(bf16)


def mp_scattered(far, near):
    other = lax.ppermute(far, "c", CORES)
    piece = near.shape[1:]
    own, *sends = pl.pallas_call(
        chip_sum_kernel,
        out_shape=(jax.ShapeDtypeStruct(piece, f32),)
        + (jax.ShapeDtypeStruct(piece, bf16),) * (RING - 1),
        in_specs=[vmem_spec()] * 2,
        out_specs=(vmem_spec(),) * RING,
        compiler_params=limits(6),
        name="chip_sum",
    )(near, other)
    came = []
    for k in (1, 3, 2):
        came.append(lax.ppermute(sends[k - 1], "y", shift(k)))
    return own, came


def split_kernel(*refs):
    ins, (send, kept) = refs[:-2], refs[-2:]
    half = send.shape[0]
    first = 0
    for keep, came in zip(ins[::2], ins[1::2]):
        columns = slice(first, first + keep.shape[1])
        send[:, columns] = (keep[:half, :].astype(f32) + came[:half, :].astype(f32)).astype(bf16)
        kept[:, columns] = (keep[half:, :].astype(f32) + came[half:, :].astype(f32)).astype(bf16)
        first += keep.shape[1]


def split_add(*pairs):
    rows = pairs[0].shape[0] // 2
    half = jax.ShapeDtypeStruct((rows, sum(a.shape[1] for a in pairs[::2])), bf16)
    return pl.pallas_call(
        split_kernel,
        out_shape=(half, half),
        in_specs=[vmem_spec()] * len(pairs),
        out_specs=(vmem_spec(),) * 2,
        compiler_params=limits(8),
        name="split_add",
    )(*pairs)


def sections(part):
    runs = []
    for p in range(RING):
        lent = LENT if p == RING - 1 else 0
        runs.append([(0, p * part + lent, part - lent), (1, p * part, part), (2, p * part, part)])
    runs[0].append((0, (RING - 1) * part, LENT))
    return runs


def finish_kernel(*refs):
    ins, outs = refs[: 2 * RING], refs[2 * RING :]
    for p, runs in enumerate(sections(outs[0].shape[1] // RING)):
        total = ins[2 * p][...].astype(f32) + ins[2 * p + 1][...].astype(f32)
        first = 0
        for out, column, width in runs:
            outs[out][:, column : column + width] = total[:, first : first + width]
            first += width


def finished(pairs, width):
    rows = pairs[0][0].shape[0]
    out = jax.ShapeDtypeStruct((rows, width), f32)
    return pl.pallas_call(
        finish_kernel,
        out_shape=(out,) * 3,
        in_specs=[vmem_spec()] * (2 * RING),
        out_specs=(vmem_spec(),) * 3,
        compiler_params=limits(6),
        name="finished",
    )(*[a for pair in pairs for a in pair])


def body(tokens, norm_gain, running_sq, gate_weight, up_weight, down_weight_t, groups, cotangent):
    tok_rows, feat = tokens.shape
    groups_total = tok_rows * RING * RING // GHOST
    coords = jnp.stack([lax.axis_index(a) for a in ("z", "x", "y", "c")]).astype(jnp.int32)
    gain = norm_gain.reshape(1, -1)
    local, both = stats(groups, coords, tokens, cotangent, groups_total)
    pieces = gathered(both)
    sums = ring_pieces(ring_sum(local, "z"), "x")
    table, quad = scale_table(sums)
    tables = gathered(table)
    (down_weight_t,) = staged(down_weight_t)
    gate_weight, up_weight = staged(gate_weight, up_weight)
    dy_full, dy_turned = cotangent_whole(coords, pieces)
    hid_full, hid_turned = normalized_whole(groups, coords, gain, pieces, tables)
    parts = []
    for p in range(RING):
        parts.append(
            hidden_part(
                p, coords, hid_full, hid_turned, dy_full, dy_turned, gate_weight, up_weight, down_weight_t
            )
        )
    last = []
    for p, (major, first) in enumerate(PATTERNS):
        minor = "x" if major == "z" else "z"
        pair = (NEAR, FAR) if first == 0 else (FAR, NEAR)
        send, keep = parts[p][3:5]
        for i, (axis, route) in enumerate(((major, 0), (major, 1), (minor, 0), (minor, 1)), 1):
            came = lax.ppermute(send, axis, pair[route])
            if i < 4:
                more = ()
                if i == 1 and p == 0:
                    more = (parts[-1][6], lax.ppermute(parts[-1][5], axis, pair[route]))
                send, keep = split_add(keep, came, *more)
        last.append((keep, came))
    grad_down_t, grad_gate, grad_up = finished(last, gate_weight.shape[1])

    far, near = back(
        coords, [[q[1] for q in parts], [q[2] for q in parts]], [gate_weight, up_weight]
    )
    kept, came = mp_scattered(far, near)
    grad, local = partials(groups, tokens, table, kept, came)
    mine, came = tok_halves(local)
    grad_tokens, grad_gain = input_grads(groups, coords, tokens, cotangent, gain, table, grad, mine, came)

    far, near = back(coords, [[q[0] for q in parts]], [down_weight_t])
    kept, came = mp_scattered(far, near)
    block_out, running_new = branch_out(tokens, running_sq.reshape(1, feat), quad, kept, came)
    return (
        block_out,
        grad_tokens,
        running_new.reshape(feat),
        grad_gain.reshape(feat),
        grad_gate,
        grad_up,
        grad_down_t,
    )


def solution(mesh):
    torus = Mesh(mesh.devices.reshape(RING, RING, RING, 2), ("z", "x", "y", "c"))
    tok, mp = ("z", "x"), ("y", "c")
    placed = (P(tok, mp), P(), P(mp), P(None, mp), P(None, mp), P(None, mp), P(tok), P(tok, mp))
    out = (P(tok, mp), P(tok, mp), P(mp), P(mp), P(tok, mp), P(tok, mp), P(tok, mp))

    return jax.shard_map(body, mesh=torus, in_specs=placed, out_specs=out, check_vma=False)
```

time: 171 us -> 187 us (1.094)
  the two profiles are of different devices: /device:TPU:16 before, /device:TPU:0 now
where the time goes in v2:
time: 187 us
  waiting for transfers between devices  84.5 us (45%)
  starting transfers between devices  60.9 us (33%)
  Pallas kernels  40.3 us (22%)
    ppermute x16, starting transfers between devices, body(): came = lax.ppermute(send, axis, pair[route])  25 us
    ppermute x6, waiting for transfers between devices, gathered(): near.append(lax.ppermute(x, 'y', shift(-k)))  19.3 us
    ppermute x1, waiting for transfers between devices, body(): more = (parts[-1][6], lax.ppermute(parts[-1][5], axis, pair[route]))  17.4 us
    pallas_call x4, Pallas kernels, hidden_part(): pl.pallas_call(hidden_kernel(p, lent), grid=(1,), out_shape=tuple((jax.Sh...  15.2 us
    ppermute x6, waiting for transfers between devices, ring_pieces(): came.append(lax.ppermute(x, axis, shift(k)))  14.3 us
    ppermute x6, waiting for transfers between devices, mp_scattered(): came.append(lax.ppermute(sends[k - 1], 'y', shift(k)))  14.2 us
    ppermute x6, starting transfers between devices, ring_pieces(): came.append(lax.ppermute(x, axis, shift(k)))  12.8 us
    ppermute x4, waiting for transfers between devices, tok_halves(): came = lax.ppermute(x, axis, pairs)  11.4 us
  transfers between devices with their start and end apart: 49, of which 17 were waited for; matrix products, arithmetic and copies ran while one was open for 0% of the time, Pallas kernels for 18%

profile of v2, /device:TPU:0, one launch (start us, length us, event | category | flops | bytes accessed | tf_op | source)
XLA Modules:
  0.0 186.9 jit_solution(1996764356144075119)
XLA Ops:
  1.9 3.2 %collective-permute-start.6 = (bf16[768,256]{1,0:T(8,128)(2,1)S(1)}, bf16[768,256]{1,0:T(8,128)(2,1)S(1)}, u32[]{:S(2)}, u32[]{:S(2)}) collective-permute-start(bf16[768,256]{1,0:T(8,128)(2,1)S(1)} %get-tuple-element.86.refs_0_), channel_id=1, source_target_pairs={{0,6},{2,0},{4,2},{6,4},{1,7},{3,1},{5,3},{7,5},{8,14},{10,8},{12,... | collective-permute-start | bytes 1179656 | tf_op jit(solution)/shard_map/ppermute | solution.py:66
  8.6 2.1 %collective-permute-start.1 = (f32[48,256]{1,0:T(8,128)S(1)}, f32[48,256]{1,0:T(8,128)S(1)}, u32[]{:S(2)}, u32[]{:S(2)}) collective-permute-start(f32[48,256]{1,0:T(8,128)S(1)} %get-tuple-element.84.refs_0_), channel_id=1, source_target_pairs={{0,96},{32,0},{64,32},{96,64},{1,97},{33,1},{65,33},{97,65},{2,98}... | collective-permute-start | bytes 147464 | tf_op jit(solution)/shard_map/ppermute | solution.py:113
  10.7 2.1 %collective-permute-done.refs_1_ = f32[48,256]{1,0:T(8,128)S(1)} collective-permute-done((f32[48,256]{1,0:T(8,128)S(1)}, f32[48,256]{1,0:T(8,128)S(1)}, u32[]{:S(2)}, u32[]{:S(2)}) %collective-permute-start) | collective-permute-done | bytes 49184 | tf_op jit(solution)/shard_map/ppermute | solution.py:113
  12.8 9.1 %collective-permute-done.6.refs_1_ = bf16[768,256]{1,0:T(8,128)(2,1)S(1)} collective-permute-done((bf16[768,256]{1,0:T(8,128)(2,1)S(1)}, bf16[768,256]{1,0:T(8,128)(2,1)S(1)}, u32[]{:S(2)}, u32[]{:S(2)}) %collective-permute-start.6) | collective-permute-done | bytes 393248 | tf_op jit(solution)/shard_map/ppermute | solution.py:66
  22.4 3.9 %collective-permute-start.2 = (f32[48,256]{1,0:T(8,128)S(1)}, f32[48,256]{1,0:T(8,128)S(1)}, u32[]{:S(2)}, u32[]{:S(2)}) collective-permute-start(f32[48,256]{1,0:T(8,128)S(1)} %get-tuple-element.84.refs_0_), channel_id=1, source_target_pairs={{0,64},{32,96},{64,0},{96,32},{1,65},{33,97},{65,1},{97,33},{2,66}... | collective-permute-start | bytes 147464 | tf_op jit(solution)/shard_map/ppermute | solution.py:113
  29.9 3.8 %collective-permute-done.3.b = f32[48,256]{1,0:T(8,128)S(1)} collective-permute-done((f32[48,256]{1,0:T(8,128)S(1)}, f32[48,256]{1,0:T(8,128)S(1)}, u32[]{:S(2)}, u32[]{:S(2)}) %collective-permute-start.3) | collective-permute-done | bytes 49184 | tf_op jit(solution)/shard_map/ppermute | solution.py:113
  35.3 2.5 %collective-permute-done.4.c = f32[48,256]{1,0:T(8,128)S(1)} collective-permute-done((f32[48,256]{1,0:T(8,128)S(1)}, f32[48,256]{1,0:T(8,128)S(1)}, u32[]{:S(2)}, u32[]{:S(2)}) %collective-permute-start.4) | collective-permute-done | bytes 49184 | tf_op jit(solution)/shard_map/ppermute | solution.py:113
  39.6 3.8 %collective-permute-done.5.d = f32[48,256]{1,0:T(8,128)S(1)} collective-permute-done((f32[48,256]{1,0:T(8,128)S(1)}, f32[48,256]{1,0:T(8,128)S(1)}, u32[]{:S(2)}, u32[]{:S(2)}) %collective-permute-start.5) | collective-permute-done | bytes 49184 | tf_op jit(solution)/shard_map/ppermute | solution.py:113
  43.4 3.8 %collective-permute-start.13 = (f32[48,256]{1,0:T(8,128)S(1)}, f32[48,256]{1,0:T(8,128)S(1)}, u32[]{:S(2)}, u32[]{:S(2)}) collective-permute-start(f32[48,256]{1,0:T(8,128)S(1)} %get-tuple-element.87.refs_8_.table), channel_id=1, source_target_pairs={{0,6},{2,0},{4,2},{6,4},{1,7},{3,1},{5,3},{7,5},{8,14},{10,8},{12,... | collective-permute-start | bytes 147464 | tf_op jit(solution)/shard_map/ppermute | solution.py:66
  50.9 3.9 %collective-permute-done.14.refs_10_ = f32[48,256]{1,0:T(8,128)S(1)} collective-permute-done((f32[48,256]{1,0:T(8,128)S(1)}, f32[48,256]{1,0:T(8,128)S(1)}, u32[]{:S(2)}, u32[]{:S(2)}) %collective-permute-start.14) | collective-permute-done | bytes 49184 | tf_op jit(solution)/shard_map/ppermute | solution.py:66
  55.6 4.6 %collective-permute-done.15.refs_11_ = f32[48,256]{1,0:T(8,128)S(1)} collective-permute-done((f32[48,256]{1,0:T(8,128)S(1)}, f32[48,256]{1,0:T(8,128)S(1)}, u32[]{:S(2)}, u32[]{:S(2)}) %collective-permute-start.15) | collective-permute-done | bytes 49184 | tf_op jit(solution)/shard_map/ppermute | solution.py:66
  61.2 2.2 %staged.3.down_w.refs_4_ = bf16[2048,1024]{1,0:T(8,128)(2,1)S(1)} custom-call(bf16[2048,1024]{1,0:T(8,128)(2,1)} %refs_0_.3), custom_call_target="tpu_custom_call" | custom-call | tf_op jit(solution)/shard_map/staged/pallas_call | solution.py:151
  63.4 3.5 %staged.2 = (bf16[2048,1024]{1,0:T(8,128)(2,1)S(1)}, bf16[2048,1024]{1,0:T(8,128)(2,1)S(1)}) custom-call(bf16[2048,1024]{1,0:T(8,128)(2,1)} %refs_0_.2, bf16[2048,1024]{1,0:T(8,128)(2,1)} %refs_1_.1), custom_call_target="tpu_custom_call" | custom-call | tf_op jit(solution)/shard_map/staged/pallas_call | solution.py:151
  69.3 3.7 %hidden_part.4 = (bf16[256,384]{1,0:T(8,128)(2,1)S(1)}, bf16[256,384]{1,0:T(8,128)(2,1)S(1)}, bf16[256,384]{1,0:T(8,128)(2,1)S(1)}, bf16[1024,768]{1,0:T(8,128)(2,1)S(1)}, bf16[1024,768]{1,0:T(8,128)(2,1)S(1)}) custom-call(s32[4]{0:T(128)S(1)} %pad_add_fusion.coords, bf16[384,2048]{1,0:T(8,128)(2,1)S(1)} %get-tuple-element.88.hid, ...), custom_call_target="tpu_custom_call" | custom-call | tf_op jit(solution)/shard_map/hidden_part/pallas_call | solution.py:392
  74.8 3.7 %hidden_part.6 = (bf16[256,384]{1,0:T(8,128)(2,1)S(1)}, bf16[256,384]{1,0:T(8,128)(2,1)S(1)}, bf16[256,384]{1,0:T(8,128)(2,1)S(1)}, bf16[1024,768]{1,0:T(8,128)(2,1)S(1)}, bf16[1024,768]{1,0:T(8,128)(2,1)S(1)}) custom-call(s32[4]{0:T(128)S(1)} %pad_add_fusion.coords, bf16[384,2048]{1,0:T(8,128)(2,1)S(1)} %get-tuple-element.88.hid, ...), custom_call_target="tpu_custom_call" | custom-call | tf_op jit(solution)/shard_map/hidden_part/pallas_call | solution.py:392
  78.9 3.7 %hidden_part.5 = (bf16[256,384]{1,0:T(8,128)(2,1)S(1)}, bf16[256,384]{1,0:T(8,128)(2,1)S(1)}, bf16[256,384]{1,0:T(8,128)(2,1)S(1)}, bf16[1024,768]{1,0:T(8,128)(2,1)S(1)}, bf16[1024,768]{1,0:T(8,128)(2,1)S(1)}) custom-call(s32[4]{0:T(128)S(1)} %pad_add_fusion.coords, bf16[384,2048]{1,0:T(8,128)(2,1)S(1)} %get-tuple-element.88.hid, ...), custom_call_target="tpu_custom_call" | custom-call | tf_op jit(solution)/shard_map/hidden_part/pallas_call | solution.py:392
  82.6 2.6 %collective-permute-start.37 = (bf16[1024,768]{1,0:T(8,128)(2,1)S(1)}, bf16[1024,768]{1,0:T(8,128)(2,1)S(1)}, u32[]{:S(2)}, u32[]{:S(2)}) collective-permute-start(bf16[1024,768]{1,0:T(8,128)(2,1)S(1)} %get-tuple-element.135), channel_id=1, source_target_pairs={{0,96},{32,64},{64,32},{96,0},{1,97},{33,65},{65,33},{97,1},{2,98}... | collective-permute-start | bytes 4718600 | tf_op jit(solution)/shard_map/ppermute | solution.py:559
  85.2 4.0 %hidden_part.7 = (bf16[256,384]{1,0:T(8,128)(2,1)S(1)}, bf16[256,384]{1,0:T(8,128)(2,1)S(1)}, bf16[256,384]{1,0:T(8,128)(2,1)S(1)}, bf16[1024,640]{1,0:T(8,128)(...) custom-call(s32[4]{0:T(128)S(1)} %pad_add_fusion.coords, ...), custom_call_target="tpu_custom_call" | custom-call | tf_op jit(solution)/shard_map/hidden_part/pallas_call | solution.py:392
  89.2 2.6 %collective-permute-start.45 = (bf16[1024,640]{1,0:T(8,128)(2,1)S(1)}, bf16[1024,640]{1,0:T(8,128)(2,1)S(1)}, u32[]{:S(2)}, u32[]{:S(2)}) collective-permute-start(bf16[1024,640]{1,0:T(8,128)(2,1)S(1)} %get-tuple-element.151), channel_id=1, source_target_pairs={{0,24},{8,16},{16,8},{24,0},{1,25},{9,17},{17,9},{25,1},{2,26},{10... | collective-permute-start | bytes 3932168 | tf_op jit(solution)/shard_map/ppermute | solution.py:559
  92.8 5.0 %back.3 = (bf16[4,256,384]{2,1,0:T(8,128)(2,1)S(1)}, bf16[4,256,384]{2,1,0:T(8,128)(2,1)S(1)}) custom-call(s32[4]{0:T(128)S(1)} %pad_add_fusion.coords, bf16[256,384]{1,0:T(8,128)(2,1)S(1)} %get-tuple-element.105.refs_0_, bf16[256,384]{1,0:T(8,128)(2,1)S(1)} %get-tuple-element.106.refs_1_, bf16[256,384]{1,0:T(8,128)(2,1)S(1)} %get-tuple-element.107.refs_2_, ...), custom_call_target="tpu_custom_call" | custom-call | tf_op jit(solution)/shard_map/back/pallas_call | solution.py:442
  97.9 17.4 %collective-permute-done.33.refs_3_ = bf16[1024,128]{1,0:T(8,128)(2,1)S(1)} collective-permute-done((bf16[1024,128]{1,0:T(8,128)(2,1)S(1)}, bf16[1024,128]{1,0:T(8,128)(2,1)S(1)}, u32[]{:S(2)}, u32[]{:S(2)}) %collective-permute-start.33) | collective-permute-done | bytes 262176 | tf_op jit(solution)/shard_map/ppermute | solution.py:563
  115.3 2.9 %back.2 = (bf16[4,256,384]{2,1,0:T(8,128)(2,1)S(1)}, bf16[4,256,384]{2,1,0:T(8,128)(2,1)S(1)}) custom-call(s32[4]{0:T(128)S(1)} %pad_add_fusion.coords, bf16[256,384]{1,0:T(8,128)(2,1)S(1)} %get-tuple-element.94.refs_0_, bf16[256,384]{1,0:T(8,128)(2,1)S(1)} %get-tuple-element.95.refs_1_, bf16[256,384]{1,0:T(8,128)(2,1)S(1)} %get-tuple-element.96.refs_2_, ...), custom_call_target="tpu_custom_call" | custom-call | tf_op jit(solution)/shard_map/back/pallas_call | solution.py:442
  119.2 3.8 %collective-permute-start.34 = (bf16[512,896]{1,0:T(8,128)(2,1)S(1)}, bf16[512,896]{1,0:T(8,128)(2,1)S(1)}, u32[]{:S(2)}, u32[]{:S(2)}) collective-permute-start(bf16[512,896]{1,0:T(8,128)(2,1)S(1)} %get-tuple-element.129), channel_id=1, source_target_pairs={{0,96},{32,64},{64,32},{96,0},{1,97},{33,65},{65,33},{97,1},{2,98}... | collective-permute-start | bytes 2752520 | tf_op jit(solution)/shard_map/ppermute | solution.py:559
  123.3 2.8 %collective-permute-start.42 = (bf16[512,768]{1,0:T(8,128)(2,1)S(1)}, bf16[512,768]{1,0:T(8,128)(2,1)S(1)}, u32[]{:S(2)}, u32[]{:S(2)}) collective-permute-start(bf16[512,768]{1,0:T(8,128)(2,1)S(1)} %get-tuple-element.145), channel_id=1, source_target_pairs={{0,24},{8,16},{16,8},{24,0},{1,25},{9,17},{17,9},{25,1},{2,26},{10... | collective-permute-start | bytes 2359304 | tf_op jit(solution)/shard_map/ppermute | solution.py:559
  127.3 7.5 %collective-permute-done.25.refs_0_ = bf16[256,384]{1,0:T(8,128)(2,1)S(1)} collective-permute-done((bf16[256,384]{1,0:T(8,128)(2,1)S(1)}, bf16[256,384]{1,0:T(8,128)(2,1)S(1)}, u32[]{:S(2)}, u32[]{:S(2)}) %collective-permute-start.25) | collective-permute-done | bytes 196640 | tf_op jit(solution)/shard_map/ppermute | solution.py:472
  135.6 7.9 %collective-permute-done.34.refs_1_ = bf16[512,896]{1,0:T(8,128)(2,1)S(1)} collective-permute-done((bf16[512,896]{1,0:T(8,128)(2,1)S(1)}, bf16[512,896]{1,0:T(8,128)(2,1)S(1)}, u32[]{:S(2)}, u32[]{:S(2)}) %collective-permute-start.34) | collective-permute-done | bytes 917536 | tf_op jit(solution)/shard_map/ppermute | solution.py:559
  147.7 5.1 %collective-permute-done.27.refs_2_ = bf16[256,384]{1,0:T(8,128)(2,1)S(1)} collective-permute-done((bf16[256,384]{1,0:T(8,128)(2,1)S(1)}, bf16[256,384]{1,0:T(8,128)(2,1)S(1)}, u32[]{:S(2)}, u32[]{:S(2)}) %collective-permute-start.27) | collective-permute-done | bytes 196640 | tf_op jit(solution)/shard_map/ppermute | solution.py:472
  152.8 2.8 %collective-permute-start.39 = (bf16[256,768]{1,0:T(8,128)(2,1)S(1)}, bf16[256,768]{1,0:T(8,128)(2,1)S(1)}, u32[]{:S(2)}, u32[]{:S(2)}) collective-permute-start(bf16[256,768]{1,0:T(8,128)(2,1)S(1)} %get-tuple-element.139), channel_id=1, source_target_pairs={{0,24},{8,16},{16,8},{24,0},{1,25},{9,17},{17,9},{25,1},{2,26},{10... | collective-permute-start | bytes 1179656 | tf_op jit(solution)/shard_map/ppermute | solution.py:559
  156.7 3.9 %collective-permute-done.28.right = f32[48,256]{1,0:T(8,128)S(1)} collective-permute-done((f32[48,256]{1,0:T(8,128)S(1)}, f32[48,256]{1,0:T(8,128)S(1)}, u32[]{:S(2)}, u32[]{:S(2)}) %collective-permute-start.28) | collective-permute-done | bytes 49184 | tf_op jit(solution)/shard_map/ppermute | solution.py:99
  160.6 2.9 %collective-permute-start.47 = (bf16[256,640]{1,0:T(8,128)(2,1)S(1)}, bf16[256,640]{1,0:T(8,128)(2,1)S(1)}, u32[]{:S(2)}, u32[]{:S(2)}) collective-permute-start(bf16[256,640]{1,0:T(8,128)(2,1)S(1)} %get-tuple-element.155), channel_id=1, source_target_pairs={{0,96},{32,64},{64,32},{96,0},{1,97},{33,65},{65,33},{97,1},{2,98}... | collective-permute-start | bytes 983048 | tf_op jit(solution)/shard_map/ppermute | solution.py:559
  163.9 5.5 %collective-permute-done.29.right = f32[48,256]{1,0:T(8,128)S(1)} collective-permute-done((f32[48,256]{1,0:T(8,128)S(1)}, f32[48,256]{1,0:T(8,128)S(1)}, u32[]{:S(2)}, u32[]{:S(2)}) %collective-permute-start.29) | collective-permute-done | bytes 49184 | tf_op jit(solution)/shard_map/ppermute | solution.py:99
  171.1 2.7 %collective-permute-start.36 = (bf16[128,896]{1,0:T(8,128)(2,1)S(1)}, bf16[128,896]{1,0:T(8,128)(2,1)S(1)}, u32[]{:S(2)}, u32[]{:S(2)}) collective-permute-start(bf16[128,896]{1,0:T(8,128)(2,1)S(1)} %get-tuple-element.133), channel_id=1, source_target_pairs={{0,24},{8,16},{16,8},{24,0},{1,25},{9,17},{17,9},{25,1},{2,26},{10... | collective-permute-start | bytes 688136 | tf_op jit(solution)/shard_map/ppermute | solution.py:559
  (107 shorter events, 47.1 us)
Async XLA Ops:
  1.9 20.0 %collective-permute-start.6 = (bf16[768,256]{1,0:T(8,128)(2,1)S(1)}, bf16[768,256]{1,0:T(8,128)(2,1)S(1)}, u32[]{:S(2)}, u32[]{:S(2)}) collective-permute-start(bf16[768,256]{1,0:T(8,128)(2,1)S(1)} %get-tuple-element.86.refs_0_), channel_id=1, source_target_pairs={{0,6},{2,0},{4,2},{6,4},{1,7},{3,1},{5,3},{7,5},{8,14},{10,8},{12,... | collective-permute-start | bytes 1179656 | tf_op jit(solution)/shard_map/ppermute | solution.py:66
  5.1 16.8 %collective-permute-start.7 = (bf16[768,256]{1,0:T(8,128)(2,1)S(1)}, bf16[768,256]{1,0:T(8,128)(2,1)S(1)}, u32[]{:S(2)}, u32[]{:S(2)}) collective-permute-start(bf16[768,256]{1,0:T(8,128)(2,1)S(1)} %get-tuple-element.86.refs_0_), channel_id=1, source_target_pairs={{0,4},{2,6},{4,0},{6,2},{1,5},{3,7},{5,1},{7,3},{8,12},{10,14},{12... | collective-permute-start | bytes 1179656 | tf_op jit(solution)/shard_map/ppermute | solution.py:66
  5.7 20.6 %collective-permute-start.8 = (bf16[768,256]{1,0:T(8,128)(2,1)S(1)}, bf16[768,256]{1,0:T(8,128)(2,1)S(1)}, u32[]{:S(2)}, u32[]{:S(2)}) collective-permute-start(bf16[768,256]{1,0:T(8,128)(2,1)S(1)} %get-tuple-element.86.refs_0_), channel_id=1, source_target_pairs={{0,2},{2,4},{4,6},{6,0},{1,3},{3,5},{5,7},{7,1},{8,10},{10,12},{12... | collective-permute-start | bytes 1179656 | tf_op jit(solution)/shard_map/ppermute | solution.py:66
  8.6 13.8 %collective-permute-start.1 = (f32[48,256]{1,0:T(8,128)S(1)}, f32[48,256]{1,0:T(8,128)S(1)}, u32[]{:S(2)}, u32[]{:S(2)}) collective-permute-start(f32[48,256]{1,0:T(8,128)S(1)} %get-tuple-element.84.refs_0_), channel_id=1, source_target_pairs={{0,96},{32,0},{64,32},{96,64},{1,97},{33,1},{65,33},{97,65},{2,98}... | collective-permute-start | bytes 147464 | tf_op jit(solution)/shard_map/ppermute | solution.py:113
  12.8 47.4 %collective-permute-start.9 = (bf16[768,256]{1,0:T(8,128)(2,1)S(1)}, bf16[768,256]{1,0:T(8,128)(2,1)S(1)}, u32[]{:S(2)}, u32[]{:S(2)}) collective-permute-start(bf16[768,256]{1,0:T(8,128)(2,1)S(1)} %get-tuple-element.86.refs_0_), channel_id=1, source_target_pairs={{0,1},{1,0},{2,3},{3,2},{4,5},{5,4},{6,7},{7,6},{8,9},{9,8},{10,11... | collective-permute-start | bytes 1179656 | tf_op jit(solution)/shard_map/ppermute | solution.py:70
  21.9 38.8 %collective-permute-start.10 = (bf16[768,256]{1,0:T(8,128)(2,1)S(1)}, bf16[768,256]{1,0:T(8,128)(2,1)S(1)}, u32[]{:S(2)}, u32[]{:S(2)}) collective-permute-start(bf16[768,256]{1,0:T(8,128)(2,1)S(1)} %collective-permute-done.6.refs_1_), channel_id=1, source_target_pairs={{0,1},{1,0},{2,3},{3,2},{4,5},{5,4},{6,7},{7,6},{8,9},{9,8},{10,11... | collective-permute-start | bytes 1179656 | tf_op jit(solution)/shard_map/ppermute | solution.py:70
  21.9 38.9 %collective-permute-start.11 = (bf16[768,256]{1,0:T(8,128)(2,1)S(1)}, bf16[768,256]{1,0:T(8,128)(2,1)S(1)}, u32[]{:S(2)}, u32[]{:S(2)}) collective-permute-start(bf16[768,256]{1,0:T(8,128)(2,1)S(1)} %collective-permute-done.7.refs_2_), channel_id=1, source_target_pairs={{0,1},{1,0},{2,3},{3,2},{4,5},{5,4},{6,7},{7,6},{8,9},{9,8},{10,11... | collective-permute-start | bytes 1179656 | tf_op jit(solution)/shard_map/ppermute | solution.py:70
  26.3 40.6 %collective-permute-start.12 = (bf16[768,256]{1,0:T(8,128)(2,1)S(1)}, bf16[768,256]{1,0:T(8,128)(2,1)S(1)}, u32[]{:S(2)}, u32[]{:S(2)}) collective-permute-start(bf16[768,256]{1,0:T(8,128)(2,1)S(1)} %collective-permute-done.8.refs_3_), channel_id=1, source_target_pairs={{0,1},{1,0},{2,3},{3,2},{4,5},{5,4},{6,7},{7,6},{8,9},{9,8},{10,11... | collective-permute-start | bytes 1179656 | tf_op jit(solution)/shard_map/ppermute | solution.py:70
  60.2 7.8 %collective-permute-start.16 = (f32[48,256]{1,0:T(8,128)S(1)}, f32[48,256]{1,0:T(8,128)S(1)}, u32[]{:S(2)}, u32[]{:S(2)}) collective-permute-start(f32[48,256]{1,0:T(8,128)S(1)} %get-tuple-element.87.refs_8_.table), channel_id=1, source_target_pairs={{0,1},{1,0},{2,3},{3,2},{4,5},{5,4},{6,7},{7,6},{8,9},{9,8},{10,11... | collective-permute-start | bytes 147464 | tf_op jit(solution)/shard_map/ppermute | solution.py:70
  60.2 7.8 %collective-permute-start.17 = (f32[48,256]{1,0:T(8,128)S(1)}, f32[48,256]{1,0:T(8,128)S(1)}, u32[]{:S(2)}, u32[]{:S(2)}) collective-permute-start(f32[48,256]{1,0:T(8,128)S(1)} %collective-permute-done.13.refs_9_), channel_id=1, source_target_pairs={{0,1},{1,0},{2,3},{3,2},{4,5},{5,4},{6,7},{7,6},{8,9},{9,8},{10,11... | collective-permute-start | bytes 147464 | tf_op jit(solution)/shard_map/ppermute | solution.py:70
  73.0 45.2 %collective-permute-start.32 = (bf16[1024,768]{1,0:T(8,128)(2,1)S(1)}, bf16[1024,768]{1,0:T(8,128)(2,1)S(1)}, u32[]{:S(2)}, u32[]{:S(2)}) collective-permute-start(bf16[1024,768]{1,0:T(8,128)(2,1)S(1)} %get-tuple-element.125), channel_id=1, source_target_pairs={{0,32},{32,0},{64,96},{96,64},{1,33},{33,1},{65,97},{97,65},{2,34}... | collective-permute-start | bytes 4718600 | tf_op jit(solution)/shard_map/ppermute | solution.py:559
  78.6 40.6 %collective-permute-start.41 = (bf16[1024,768]{1,0:T(8,128)(2,1)S(1)}, bf16[1024,768]{1,0:T(8,128)(2,1)S(1)}, u32[]{:S(2)}, u32[]{:S(2)}) collective-permute-start(bf16[1024,768]{1,0:T(8,128)(2,1)S(1)} %get-tuple-element.143), channel_id=1, source_target_pairs={{0,8},{8,0},{16,24},{24,16},{1,9},{9,1},{17,25},{25,17},{2,10},{10... | collective-permute-start | bytes 4718600 | tf_op jit(solution)/shard_map/ppermute | solution.py:559
  82.6 40.7 %collective-permute-start.37 = (bf16[1024,768]{1,0:T(8,128)(2,1)S(1)}, bf16[1024,768]{1,0:T(8,128)(2,1)S(1)}, u32[]{:S(2)}, u32[]{:S(2)}) collective-permute-start(bf16[1024,768]{1,0:T(8,128)(2,1)S(1)} %get-tuple-element.135), channel_id=1, source_target_pairs={{0,96},{32,64},{64,32},{96,0},{1,97},{33,65},{65,33},{97,1},{2,98}... | collective-permute-start | bytes 4718600 | tf_op jit(solution)/shard_map/ppermute | solution.py:559
  89.2 37.3 %collective-permute-start.45 = (bf16[1024,640]{1,0:T(8,128)(2,1)S(1)}, bf16[1024,640]{1,0:T(8,128)(2,1)S(1)}, u32[]{:S(2)}, u32[]{:S(2)}) collective-permute-start(bf16[1024,640]{1,0:T(8,128)(2,1)S(1)} %get-tuple-element.151), channel_id=1, source_target_pairs={{0,24},{8,16},{16,8},{24,0},{1,25},{9,17},{17,9},{25,1},{2,26},{10... | collective-permute-start | bytes 3932168 | tf_op jit(solution)/shard_map/ppermute | solution.py:559
  91.8 23.4 %collective-permute-start.33 = (bf16[1024,128]{1,0:T(8,128)(2,1)S(1)}, bf16[1024,128]{1,0:T(8,128)(2,1)S(1)}, u32[]{:S(2)}, u32[]{:S(2)}) collective-permute-start(bf16[1024,128]{1,0:T(8,128)(2,1)S(1)} %get-tuple-element.127), channel_id=1, source_target_pairs={{0,32},{32,0},{64,96},{96,64},{1,33},{33,1},{65,97},{97,65},{2,34}... | collective-permute-start | bytes 786440 | tf_op jit(solution)/shard_map/ppermute | solution.py:563
  115.3 11.7 %collective-permute-start.24 = (bf16[4,256,384]{2,1,0:T(8,128)(2,1)S(1)}, bf16[4,256,384]{2,1,0:T(8,128)(2,1)S(1)}, u32[]{:S(2)}, u32[]{:S(2)}) collective-permute-start(bf16[4,256,384]{2,1,0:T(8,128)(2,1)S(1)} %get-tuple-element.114), channel_id=1, source_target_pairs={{0,1},{1,0},{2,3},{3,2},{4,5},{5,4},{6,7},{7,6},{8,9},{9,8},{10,11... | collective-permute-start | bytes 2359304 | tf_op jit(solution)/shard_map/ppermute | solution.py:459
  118.1 9.1 %collective-permute-start.20 = (bf16[4,256,384]{2,1,0:T(8,128)(2,1)S(1)}, bf16[4,256,384]{2,1,0:T(8,128)(2,1)S(1)}, u32[]{:S(2)}, u32[]{:S(2)}) collective-permute-start(bf16[4,256,384]{2,1,0:T(8,128)(2,1)S(1)} %get-tuple-element.99), channel_id=1, source_target_pairs={{0,1},{1,0},{2,3},{3,2},{4,5},{5,4},{6,7},{7,6},{8,9},{9,8},{10,11... | collective-permute-start | bytes 2359304 | tf_op jit(solution)/shard_map/ppermute | solution.py:459
  119.2 24.3 %collective-permute-start.34 = (bf16[512,896]{1,0:T(8,128)(2,1)S(1)}, bf16[512,896]{1,0:T(8,128)(2,1)S(1)}, u32[]{:S(2)}, u32[]{:S(2)}) collective-permute-start(bf16[512,896]{1,0:T(8,128)(2,1)S(1)} %get-tuple-element.129), channel_id=1, source_target_pairs={{0,96},{32,64},{64,32},{96,0},{1,97},{33,65},{65,33},{97,1},{2,98}... | collective-permute-start | bytes 2752520 | tf_op jit(solution)/shard_map/ppermute | solution.py:559
  123.3 22.1 %collective-permute-start.42 = (bf16[512,768]{1,0:T(8,128)(2,1)S(1)}, bf16[512,768]{1,0:T(8,128)(2,1)S(1)}, u32[]{:S(2)}, u32[]{:S(2)}) collective-permute-start(bf16[512,768]{1,0:T(8,128)(2,1)S(1)} %get-tuple-element.145), channel_id=1, source_target_pairs={{0,24},{8,16},{16,8},{24,0},{1,25},{9,17},{17,9},{25,1},{2,26},{10... | collective-permute-start | bytes 2359304 | tf_op jit(solution)/shard_map/ppermute | solution.py:559
  126.5 20.9 %collective-permute-start.38 = (bf16[512,768]{1,0:T(8,128)(2,1)S(1)}, bf16[512,768]{1,0:T(8,128)(2,1)S(1)}, u32[]{:S(2)}, u32[]{:S(2)}) collective-permute-start(bf16[512,768]{1,0:T(8,128)(2,1)S(1)} %get-tuple-element.137), channel_id=1, source_target_pairs={{0,32},{32,0},{64,96},{96,64},{1,33},{33,1},{65,97},{97,65},{2,34}... | collective-permute-start | bytes 2359304 | tf_op jit(solution)/shard_map/ppermute | solution.py:559
  126.9 29.5 %collective-permute-start.46 = (bf16[512,640]{1,0:T(8,128)(2,1)S(1)}, bf16[512,640]{1,0:T(8,128)(2,1)S(1)}, u32[]{:S(2)}, u32[]{:S(2)}) collective-permute-start(bf16[512,640]{1,0:T(8,128)(2,1)S(1)} %get-tuple-element.153), channel_id=1, source_target_pairs={{0,8},{8,0},{16,24},{24,16},{1,9},{9,1},{17,25},{25,17},{2,10},{10... | collective-permute-start | bytes 1966088 | tf_op jit(solution)/shard_map/ppermute | solution.py:559
  134.8 10.1 %collective-permute-start.26 = (bf16[256,384]{1,0:T(8,128)(2,1)S(1)}, bf16[256,384]{1,0:T(8,128)(2,1)S(1)}, u32[]{:S(2)}, u32[]{:S(2)}) collective-permute-start(bf16[256,384]{1,0:T(8,128)(2,1)S(1)} %get-tuple-element.117), channel_id=1, source_target_pairs={{0,6},{2,0},{4,2},{6,4},{1,7},{3,1},{5,3},{7,5},{8,14},{10,8},{12,... | collective-permute-start | bytes 589832 | tf_op jit(solution)/shard_map/ppermute | solution.py:472
  143.5 9.3 %collective-permute-start.27 = (bf16[256,384]{1,0:T(8,128)(2,1)S(1)}, bf16[256,384]{1,0:T(8,128)(2,1)S(1)}, u32[]{:S(2)}, u32[]{:S(2)}) collective-permute-start(bf16[256,384]{1,0:T(8,128)(2,1)S(1)} %get-tuple-element.118), channel_id=1, source_target_pairs={{0,4},{2,6},{4,0},{6,2},{1,5},{3,7},{5,1},{7,3},{8,12},{10,14},{12... | collective-permute-start | bytes 589832 | tf_op jit(solution)/shard_map/ppermute | solution.py:472
  144.8 26.1 %collective-permute-start.35 = (bf16[256,896]{1,0:T(8,128)(2,1)S(1)}, bf16[256,896]{1,0:T(8,128)(2,1)S(1)}, u32[]{:S(2)}, u32[]{:S(2)}) collective-permute-start(bf16[256,896]{1,0:T(8,128)(2,1)S(1)} %get-tuple-element.131), channel_id=1, source_target_pairs={{0,8},{8,0},{16,24},{24,16},{1,9},{9,1},{17,25},{25,17},{2,10},{10... | collective-permute-start | bytes 1376264 | tf_op jit(solution)/shard_map/ppermute | solution.py:559
  145.4 18.1 %collective-permute-start.21 = (bf16[256,384]{1,0:T(8,128)(2,1)S(1)}, bf16[256,384]{1,0:T(8,128)(2,1)S(1)}, u32[]{:S(2)}, u32[]{:S(2)}) collective-permute-start(bf16[256,384]{1,0:T(8,128)(2,1)S(1)} %get-tuple-element.101), channel_id=1, source_target_pairs={{0,2},{2,4},{4,6},{6,0},{1,3},{3,5},{5,7},{7,1},{8,10},{10,12},{12... | collective-permute-start | bytes 589832 | tf_op jit(solution)/shard_map/ppermute | solution.py:472
  147.4 23.6 %collective-permute-start.43 = (bf16[256,768]{1,0:T(8,128)(2,1)S(1)}, bf16[256,768]{1,0:T(8,128)(2,1)S(1)}, u32[]{:S(2)}, u32[]{:S(2)}) collective-permute-start(bf16[256,768]{1,0:T(8,128)(2,1)S(1)} %get-tuple-element.147), channel_id=1, source_target_pairs={{0,32},{32,0},{64,96},{96,64},{1,33},{33,1},{65,97},{97,65},{2,34}... | collective-permute-start | bytes 1179656 | tf_op jit(solution)/shard_map/ppermute | solution.py:559
  152.8 21.0 %collective-permute-start.39 = (bf16[256,768]{1,0:T(8,128)(2,1)S(1)}, bf16[256,768]{1,0:T(8,128)(2,1)S(1)}, u32[]{:S(2)}, u32[]{:S(2)}) collective-permute-start(bf16[256,768]{1,0:T(8,128)(2,1)S(1)} %get-tuple-element.139), channel_id=1, source_target_pairs={{0,24},{8,16},{16,8},{24,0},{1,25},{9,17},{17,9},{25,1},{2,26},{10... | collective-permute-start | bytes 1179656 | tf_op jit(solution)/shard_map/ppermute | solution.py:559
  160.6 17.4 %collective-permute-start.47 = (bf16[256,640]{1,0:T(8,128)(2,1)S(1)}, bf16[256,640]{1,0:T(8,128)(2,1)S(1)}, u32[]{:S(2)}, u32[]{:S(2)}) collective-permute-start(bf16[256,640]{1,0:T(8,128)(2,1)S(1)} %get-tuple-element.155), channel_id=1, source_target_pairs={{0,96},{32,64},{64,32},{96,0},{1,97},{33,65},{65,33},{97,1},{2,98}... | collective-permute-start | bytes 983048 | tf_op jit(solution)/shard_map/ppermute | solution.py:559
  170.9 7.8 %collective-permute-start.23 = (bf16[256,384]{1,0:T(8,128)(2,1)S(1)}, bf16[256,384]{1,0:T(8,128)(2,1)S(1)}, u32[]{:S(2)}, u32[]{:S(2)}) collective-permute-start(bf16[256,384]{1,0:T(8,128)(2,1)S(1)} %get-tuple-element.103), channel_id=1, source_target_pairs={{0,4},{2,6},{4,0},{6,2},{1,5},{3,7},{5,1},{7,3},{8,12},{10,14},{12... | collective-permute-start | bytes 589832 | tf_op jit(solution)/shard_map/ppermute | solution.py:472
  171.1 14.6 %collective-permute-start.36 = (bf16[128,896]{1,0:T(8,128)(2,1)S(1)}, bf16[128,896]{1,0:T(8,128)(2,1)S(1)}, u32[]{:S(2)}, u32[]{:S(2)}) collective-permute-start(bf16[128,896]{1,0:T(8,128)(2,1)S(1)} %get-tuple-element.133), channel_id=1, source_target_pairs={{0,24},{8,16},{16,8},{24,0},{1,25},{9,17},{17,9},{25,1},{2,26},{10... | collective-permute-start | bytes 688136 | tf_op jit(solution)/shard_map/ppermute | solution.py:559
  176.6 9.0 %collective-permute-start.44 = (bf16[128,768]{1,0:T(8,128)(2,1)S(1)}, bf16[128,768]{1,0:T(8,128)(2,1)S(1)}, u32[]{:S(2)}, u32[]{:S(2)}) collective-permute-start(bf16[128,768]{1,0:T(8,128)(2,1)S(1)} %get-tuple-element.149), channel_id=1, source_target_pairs={{0,96},{32,64},{64,32},{96,0},{1,97},{33,65},{65,33},{97,1},{2,98}... | collective-permute-start | bytes 589832 | tf_op jit(solution)/shard_map/ppermute | solution.py:559
  178.0 7.6 %collective-permute-start.40 = (bf16[128,768]{1,0:T(8,128)(2,1)S(1)}, bf16[128,768]{1,0:T(8,128)(2,1)S(1)}, u32[]{:S(2)}, u32[]{:S(2)}) collective-permute-start(bf16[128,768]{1,0:T(8,128)(2,1)S(1)} %get-tuple-element.141), channel_id=1, source_target_pairs={{0,8},{8,0},{16,24},{24,16},{1,9},{9,1},{17,25},{25,17},{2,10},{10... | collective-permute-start | bytes 589832 | tf_op jit(solution)/shard_map/ppermute | solution.py:559
  (20 other events, 119.2 us)

commit v3 on v2

--- a/solution.py
+++ b/solution.py
@@ -205,9 +205,10 @@
 
 def partial_kernel(groups, tokens, table, own, *refs):
     came, (grad, out) = refs[:-2], refs[-2:]
-    total = own[...]
+    feat = tokens.shape[1]
+    total = own[:feat, :]
     for ref in came:
-        total = total + ref[...].astype(f32)
+        total = total + ref[:feat, :].astype(f32)
     grad[...] = total.T
     out[...] = jnp.zeros_like(out)
     for b in range(tokens.shape[0] // BLK):
@@ -264,9 +265,10 @@
 
 def branch_kernel(tokens, running, quad, own, *refs):
     came, (out, running_new) = refs[:-2], refs[-2:]
-    total = own[...]
+    feat = tokens.shape[1]
+    total = own[feat:, :]
     for ref in came:
-        total = total + ref[...].astype(f32)
+        total = total + ref[feat:, :].astype(f32)
     out[...] = (tokens[...].astype(f32) + total.T).astype(bf16)
     mean = jnp.sum(quad[...], axis=0, keepdims=True) / quad.shape[0]
     running_new[...] = (1.0 - MOMENTUM) * running[...] + MOMENTUM * mean
@@ -345,14 +347,20 @@
     )(in_hbm(groups), coords, gain, *pieces, *tables)
 
 
-def rows_product(blocks, turned, right, send, keep, first):
+def rows_product(blocks, turned, right, outs, first):
     columns = slice(first, first + right.shape[1])
     half = len(blocks) // 2
-    for part, out in ((blocks[:half], send), (blocks[half:], keep)):
+    values = []
+    for part in (blocks[:half], blocks[half:]):
         left = jnp.concatenate(
             [turned[pl.ds(pl.multiple_of(b * 128, 128), 128), :] for b in part], axis=0
         )
-        out[:, columns] = jnp.dot(left, right, preferred_element_type=f32).astype(out.dtype)
+        values.append(jnp.dot(left, right, preferred_element_type=f32).astype(bf16))
+    done = 0
+    for out in outs:
+        value, start = values[done // values[0].shape[0]], done % values[0].shape[0]
+        out[:, columns] = value[start : start + out.shape[0], :]
+        done += out.shape[0]
 
 
 def hidden_kernel(p, lent):
@@ -366,11 +374,11 @@
         ggi = (grad * lift * sigma * (1.0 + gate * (1.0 - sigma))).astype(bf16)
         gl = (grad * act).astype(bf16)
         own = row_blocks(coords, PATTERNS[p])
-        rows_product(own, dy_t, hidden[:, lent:], outs[0], outs[1], 0)
+        rows_product(own, dy_t, hidden[:, lent:], outs[:3], 0)
         both = jnp.concatenate([ggi, gl], axis=1)
-        rows_product(own, hid_t, both, outs[0], outs[1], hidden.shape[1] - lent)
+        rows_product(own, hid_t, both, outs[:3], hidden.shape[1] - lent)
         if lent:
-            rows_product(row_blocks(coords, PATTERNS[0]), dy_t, hidden[:, :lent], outs[2], outs[3], 0)
+            rows_product(row_blocks(coords, PATTERNS[0]), dy_t, hidden[:, :lent], outs[3:], 0)
         hidden_t[...] = hidden.T
         ggi_t[...] = ggi.T
         gl_t[...] = gl.T
@@ -387,8 +395,9 @@
         return pl.BlockSpec(shape, lambda i: (0, 0))
 
     weight = pl.BlockSpec((width, part), lambda i: (0, p))
-    halves = [3 * part - lent] * 2 + ([lent] * 2 if lent else [])
-    shapes = [(part, rows)] * 3 + [(width // 2, n) for n in halves]
+    columns = 3 * part - lent
+    shapes = [(part, rows)] * 3 + [(width // 4, columns)] * 2 + [(width // 2, columns)]
+    shapes += [(width // 2, lent)] * 2 if lent else []
     return pl.pallas_call(
         hidden_kernel(p, lent),
         grid=(1,),
@@ -409,62 +418,62 @@
     )(coords, hid, hid_t, dy, dy_t, gate_w, up_w, down_w)
 
 
-def back_kernel(pairs):
-    def kernel(coords, *refs):
-        acts = refs[: pairs * RING]
-        weights = refs[pairs * RING : pairs * RING + pairs]
-        outs = refs[pairs * RING + pairs :]
-        feat = outs[0].shape[1]
-        for other, out in ((1, outs[0]), (0, outs[1])):
-            total = None
-            for j in range(pairs):
-                act = jnp.concatenate([r[...] for r in acts[j * RING : (j + 1) * RING]], axis=0)
-                left = jnp.concatenate(
-                    [
-                        weights[j][pl.ds(pl.multiple_of(b * feat, feat), feat), :]
-                        for b in feature_blocks(coords, other)
-                    ],
-                    axis=0,
-                )
-                term = jnp.dot(left, act, preferred_element_type=f32)
-                total = term if total is None else total + term
+def back_kernel(coords, *refs):
+    acts, weights, outs = refs[: 3 * RING], refs[3 * RING : 3 * RING + 3], refs[3 * RING + 3 :]
+    feat = outs[0].shape[1]
+    whole = [
+        jnp.concatenate([r[...] for r in acts[j * RING : (j + 1) * RING]], axis=0) for j in range(3)
+    ]
+    for other, out in ((1, outs[0]), (0, outs[1])):
+        terms = []
+        for weight, act in zip(weights, whole):
+            left = jnp.concatenate(
+                [
+                    weight[pl.ds(pl.multiple_of(b * feat, feat), feat), :]
+                    for b in feature_blocks(coords, other)
+                ],
+                axis=0,
+            )
+            terms.append(jnp.dot(left, act, preferred_element_type=f32))
+        for j, total in enumerate((terms[0] + terms[1], terms[2])):
             for k in range(RING):
-                out[k] = total[k * feat : (k + 1) * feat, :].astype(bf16)
-
-    return kernel
+                out[j * RING + k] = total[k * feat : (k + 1) * feat, :].astype(bf16)
 
 
 def back(coords, acts, weights):
     rows = acts[0][0].shape[1]
     feat = weights[0].shape[0] // (2 * RING)
-    pairs = len(weights)
-    out = jax.ShapeDtypeStruct((RING, feat, rows), bf16)
-    return pl.pallas_call(
-        back_kernel(pairs),
-        in_specs=[smem_spec()] + [vmem_spec()] * (pairs * RING + pairs),
+    out = jax.ShapeDtypeStruct((2 * RING, feat, rows), bf16)
+    return pl.pallas_call(
+        back_kernel,
+        in_specs=[smem_spec()] + [vmem_spec()] * (3 * RING + 3),
         out_specs=(vmem_spec(), vmem_spec()),
         out_shape=(out, out),
-        compiler_params=limits(20),
+        compiler_params=limits(24),
         name="back",
     )(coords, *[a for group in acts for a in group], *weights)
 
 
 def chip_sum_kernel(near, other, own, *sends):
-    own[...] = near[0].astype(f32) + other[0].astype(f32)
-    for k, send in enumerate(sends, 1):
-        send[...] = (near[k].astype(f32) + other[k].astype(f32)).astype(bf16)
+    feat = near.shape[1]
+    for j in range(2):
+        rows = slice(j * feat, (j + 1) * feat)
+        own[rows, :] = near[j * RING].astype(f32) + other[j * RING].astype(f32)
+        for k, send in enumerate(sends, 1):
+            i = j * RING + k
+            send[rows, :] = (near[i].astype(f32) + other[i].astype(f32)).astype(bf16)
 
 
 def mp_scattered(far, near):
     other = lax.ppermute(far, "c", CORES)
-    piece = near.shape[1:]
+    piece = (2 * near.shape[1], near.shape[2])
     own, *sends = pl.pallas_call(
         chip_sum_kernel,
         out_shape=(jax.ShapeDtypeStruct(piece, f32),)
         + (jax.ShapeDtypeStruct(piece, bf16),) * (RING - 1),
         in_specs=[vmem_spec()] * 2,
         out_specs=(vmem_spec(),) * RING,
-        compiler_params=limits(6),
+        compiler_params=limits(8),
         name="chip_sum",
     )(near, other)
     came = []
@@ -494,6 +503,34 @@
         out_specs=(vmem_spec(),) * 2,
         compiler_params=limits(8),
         name="split_add",
+    )(*pairs)
+
+
+def half_kernel(half):
+    def kernel(*refs):
+        ins, out = refs[:-1], refs[-1]
+        rows = out.shape[0]
+        first = 0
+        for keep, came in zip(ins[::2], ins[1::2]):
+            mine = keep[half * rows : (half + 1) * rows, :]
+            start = half * rows if came.shape[0] > rows else 0
+            theirs = came[start : start + rows, :]
+            columns = slice(first, first + keep.shape[1])
+            out[:, columns] = (mine.astype(f32) + theirs.astype(f32)).astype(bf16)
+            first += keep.shape[1]
+
+    return kernel
+
+
+def half_add(half, *pairs):
+    out = jax.ShapeDtypeStruct((pairs[0].shape[0] // 2, sum(a.shape[1] for a in pairs[::2])), bf16)
+    return pl.pallas_call(
+        half_kernel(half),
+        out_shape=out,
+        in_specs=[vmem_spec()] * len(pairs),
+        out_specs=vmem_spec(),
+        compiler_params=limits(6),
+        name="half_add",
     )(*pairs)
 
 
@@ -554,28 +591,32 @@
     for p, (major, first) in enumerate(PATTERNS):
         minor = "x" if major == "z" else "z"
         pair = (NEAR, FAR) if first == 0 else (FAR, NEAR)
-        send, keep = parts[p][3:5]
-        for i, (axis, route) in enumerate(((major, 0), (major, 1), (minor, 0), (minor, 1)), 1):
-            came = lax.ppermute(send, axis, pair[route])
-            if i < 4:
-                more = ()
-                if i == 1 and p == 0:
-                    more = (parts[-1][6], lax.ppermute(parts[-1][5], axis, pair[route]))
-                send, keep = split_add(keep, came, *more)
+        send_a, send_b, keep = parts[p][3:6]
+        more = ()
+        if p == 0:
+            more = (parts[-1][7], lax.ppermute(parts[-1][6], major, pair[0]))
+        came_a = lax.ppermute(send_a, major, pair[0])
+        came_b = lax.ppermute(send_b, major, pair[0])
+        send = half_add(0, keep, came_a, *more)
+        came = lax.ppermute(send, major, pair[1])
+        keep = half_add(1, keep, came_b, *more)
+        for route in (0, 1):
+            send, keep = split_add(keep, came)
+            came = lax.ppermute(send, minor, pair[route])
         last.append((keep, came))
     grad_down_t, grad_gate, grad_up = finished(last, gate_weight.shape[1])
 
     far, near = back(
-        coords, [[q[1] for q in parts], [q[2] for q in parts]], [gate_weight, up_weight]
+        coords,
+        [[q[1] for q in parts], [q[2] for q in parts], [q[0] for q in parts]],
+        [gate_weight, up_weight, down_weight_t],
     )
-    kept, came = mp_scattered(far, near)
-    grad, local = partials(groups, tokens, table, kept, came)
+    kept, came_y = mp_scattered(far, near)
+    grad, local = partials(groups, tokens, table, kept, came_y)
     mine, came = tok_halves(local)
     grad_tokens, grad_gain = input_grads(groups, coords, tokens, cotangent, gain, table, grad, mine, came)
 
-    far, near = back(coords, [[q[0] for q in parts]], [down_weight_t])
-    kept, came = mp_scattered(far, near)
-    block_out, running_new = branch_out(tokens, running_sq.reshape(1, feat), quad, kept, came)
+    block_out, running_new = branch_out(tokens, running_sq.reshape(1, feat), quad, kept, came_y)
     return (
         block_out,
         grad_tokens,

time: 187 us -> 217 us (1.16)
  the two profiles are of different devices: /device:TPU:0 before, /device:TPU:24 now
where the time goes in v3:
time: 217 us; the launch traced here: 216 us
  waiting for transfers between devices  120 us (55%)
  starting transfers between devices  55.9 us (26%)
  Pallas kernels  39.7 us (18%)
    ppermute x4, waiting for transfers between devices, body(): came_b = lax.ppermute(send_b, major, pair[0])  33.5 us
    ppermute x6, waiting for transfers between devices, gathered(): near.append(lax.ppermute(x, 'y', shift(-k)))  25.3 us
    pallas_call x4, Pallas kernels, hidden_part(): pl.pallas_call(hidden_kernel(p, lent), grid=(1,), out_shape=tuple((jax.Sh...  15.2 us
    ppermute x6, waiting for transfers between devices, ring_pieces(): came.append(lax.ppermute(x, axis, shift(k)))  14.3 us
    ppermute x6, starting transfers between devices, ring_pieces(): came.append(lax.ppermute(x, axis, shift(k)))  12.8 us
    ppermute x4, waiting for transfers between devices, body(): came = lax.ppermute(send, major, pair[1])  11.4 us
    ppermute x8, starting transfers between devices, body(): came = lax.ppermute(send, minor, pair[route])  9.38 us
    ppermute x4, waiting for transfers between devices, tok_halves(): came = lax.ppermute(x, axis, pairs)  8.93 us
  transfers between devices with their start and end apart: 49, of which 20 were waited for; matrix products, arithmetic and copies ran while one was open for 0% of the time, Pallas kernels for 15%

profile of v3, /device:TPU:24, one launch (start us, length us, event | category | flops | bytes accessed | tf_op | source)
XLA Modules:
  0.0 216.3 jit_solution(4208367333127653496)
XLA Ops:
  11.9 10.5 %collective-permute-done.6.refs_1_ = bf16[768,256]{1,0:T(8,128)(2,1)S(1)} collective-permute-done((bf16[768,256]{1,0:T(8,128)(2,1)S(1)}, bf16[768,256]{1,0:T(8,128)(2,1)S(1)}, u32[]{:S(2)}, u32[]{:S(2)}) %collective-permute-start.6) | collective-permute-done | bytes 393248 | tf_op jit(solution)/shard_map/ppermute | solution.py:66
  23.0 3.9 %collective-permute-start.2 = (f32[48,256]{1,0:T(8,128)S(1)}, f32[48,256]{1,0:T(8,128)S(1)}, u32[]{:S(2)}, u32[]{:S(2)}) collective-permute-start(f32[48,256]{1,0:T(8,128)S(1)} %get-tuple-element.74.refs_0_), channel_id=1, source_target_pairs={{0,64},{32,96},{64,0},{96,32},{1,65},{33,97},{65,1},{97,33},{2,66}... | collective-permute-start | bytes 147464 | tf_op jit(solution)/shard_map/ppermute | solution.py:113
  30.5 3.8 %collective-permute-done.3.b = f32[48,256]{1,0:T(8,128)S(1)} collective-permute-done((f32[48,256]{1,0:T(8,128)S(1)}, f32[48,256]{1,0:T(8,128)S(1)}, u32[]{:S(2)}, u32[]{:S(2)}) %collective-permute-start.3) | collective-permute-done | bytes 49184 | tf_op jit(solution)/shard_map/ppermute | solution.py:113
  35.8 2.5 %collective-permute-done.4.c = f32[48,256]{1,0:T(8,128)S(1)} collective-permute-done((f32[48,256]{1,0:T(8,128)S(1)}, f32[48,256]{1,0:T(8,128)S(1)}, u32[]{:S(2)}, u32[]{:S(2)}) %collective-permute-start.4) | collective-permute-done | bytes 49184 | tf_op jit(solution)/shard_map/ppermute | solution.py:113
  40.2 3.8 %collective-permute-done.5.d = f32[48,256]{1,0:T(8,128)S(1)} collective-permute-done((f32[48,256]{1,0:T(8,128)S(1)}, f32[48,256]{1,0:T(8,128)S(1)}, u32[]{:S(2)}, u32[]{:S(2)}) %collective-permute-start.5) | collective-permute-done | bytes 49184 | tf_op jit(solution)/shard_map/ppermute | solution.py:113
  44.1 5.3 %collective-permute-done.13.refs_9_ = f32[48,256]{1,0:T(8,128)S(1)} collective-permute-done((f32[48,256]{1,0:T(8,128)S(1)}, f32[48,256]{1,0:T(8,128)S(1)}, u32[]{:S(2)}, u32[]{:S(2)}) %collective-permute-start.13) | collective-permute-done | bytes 49184 | tf_op jit(solution)/shard_map/ppermute | solution.py:66
  49.6 5.4 %collective-permute-done.14.refs_10_ = f32[48,256]{1,0:T(8,128)S(1)} collective-permute-done((f32[48,256]{1,0:T(8,128)S(1)}, f32[48,256]{1,0:T(8,128)S(1)}, u32[]{:S(2)}, u32[]{:S(2)}) %collective-permute-start.14) | collective-permute-done | bytes 49184 | tf_op jit(solution)/shard_map/ppermute | solution.py:66
  55.0 4.1 %collective-permute-done.15.refs_11_ = f32[48,256]{1,0:T(8,128)S(1)} collective-permute-done((f32[48,256]{1,0:T(8,128)S(1)}, f32[48,256]{1,0:T(8,128)S(1)}, u32[]{:S(2)}, u32[]{:S(2)}) %collective-permute-start.15) | collective-permute-done | bytes 49184 | tf_op jit(solution)/shard_map/ppermute | solution.py:66
  62.3 3.5 %staged.2 = (bf16[2048,1024]{1,0:T(8,128)(2,1)S(1)}, bf16[2048,1024]{1,0:T(8,128)(2,1)S(1)}) custom-call(bf16[2048,1024]{1,0:T(8,128)(2,1)} %refs_0_.2, bf16[2048,1024]{1,0:T(8,128)(2,1)} %refs_1_.1), custom_call_target="tpu_custom_call" | custom-call | tf_op jit(solution)/shard_map/staged/pallas_call | solution.py:151
  68.2 4.0 %hidden_part.7 = (bf16[256,384]{1,0:T(8,128)(2,1)S(1)}, bf16[256,384]{1,0:T(8,128)(2,1)S(1)}, bf16[256,384]{1,0:T(8,128)(2,1)S(1)}, bf16[512,640]{1,0:T(8,128)(2...) custom-call(s32[4]{0:T(128)S(1)} %pad_add_fusion.coords, ...), custom_call_target="tpu_custom_call" | custom-call | tf_op jit(solution)/shard_map/hidden_part/pallas_call | solution.py:401
  72.2 3.0 %collective-permute-start.45 = (bf16[512,640]{1,0:T(8,128)(2,1)S(1)}, bf16[512,640]{1,0:T(8,128)(2,1)S(1)}, u32[]{:S(2)}, u32[]{:S(2)}) collective-permute-start(bf16[512,640]{1,0:T(8,128)(2,1)S(1)} %get-tuple-element.133), channel_id=1, source_target_pairs={{0,24},{8,16},{16,8},{24,0},{1,25},{9,17},{17,9},{25,1},{2,26},{10... | collective-permute-start | bytes 1966088 | tf_op jit(solution)/shard_map/ppermute | solution.py:598
  75.2 3.7 %hidden_part.4 = (bf16[256,384]{1,0:T(8,128)(2,1)S(1)}, bf16[256,384]{1,0:T(8,128)(2,1)S(1)}, bf16[256,384]{1,0:T(8,128)(2,1)S(1)}, bf16[512,768]{1,0:T(8,128)(2...) custom-call(s32[4]{0:T(128)S(1)} %pad_add_fusion.coords, ...), custom_call_target="tpu_custom_call" | custom-call | tf_op jit(solution)/shard_map/hidden_part/pallas_call | solution.py:401
  81.0 3.7 %hidden_part.6 = (bf16[256,384]{1,0:T(8,128)(2,1)S(1)}, bf16[256,384]{1,0:T(8,128)(2,1)S(1)}, bf16[256,384]{1,0:T(8,128)(2,1)S(1)}, bf16[512,768]{1,0:T(8,128)(2...) custom-call(s32[4]{0:T(128)S(1)} %pad_add_fusion.coords, ...), custom_call_target="tpu_custom_call" | custom-call | tf_op jit(solution)/shard_map/hidden_part/pallas_call | solution.py:401
  84.8 3.7 %hidden_part.5 = (bf16[256,384]{1,0:T(8,128)(2,1)S(1)}, bf16[256,384]{1,0:T(8,128)(2,1)S(1)}, bf16[256,384]{1,0:T(8,128)(2,1)S(1)}, bf16[512,768]{1,0:T(8,128)(2...) custom-call(s32[4]{0:T(128)S(1)} %pad_add_fusion.coords, ...), custom_call_target="tpu_custom_call" | custom-call | tf_op jit(solution)/shard_map/hidden_part/pallas_call | solution.py:401
  88.5 7.2 %back.1 = (bf16[8,256,384]{2,1,0:T(8,128)(2,1)S(1)}, bf16[8,256,384]{2,1,0:T(8,128)(2,1)S(1)}) custom-call(s32[4]{0:T(128)S(1)} %pad_add_fusion.coords, bf16[256,384]{1,0:T(8,128)(2,1)S(1)} %get-tuple-element.84.refs_0_, bf16[256,384]{1,0:T(8,128)(2,1)S(1)} %get-tuple-element.85.refs_1_, bf16[256,384]{1,0:T(8,128)(2,1)S(1)} %get-tuple-element.86.refs_2_, ...), custom_call_target="tpu_custom_call" | custom-call | tf_op jit(solution)/shard_map/back/pallas_call | solution.py:447
  96.4 7.5 %collective-permute-done.29.refs_3_ = bf16[1024,128]{1,0:T(8,128)(2,1)S(1)} collective-permute-done((bf16[1024,128]{1,0:T(8,128)(2,1)S(1)}, bf16[1024,128]{1,0:T(8,128)(2,1)S(1)}, u32[]{:S(2)}, u32[]{:S(2)}) %collective-permute-start.29) | collective-permute-done | bytes 262176 | tf_op jit(solution)/shard_map/ppermute | solution.py:597
  105.9 8.3 %collective-permute-done.44.refs_1_ = bf16[512,640]{1,0:T(8,128)(2,1)S(1)} collective-permute-done((bf16[512,640]{1,0:T(8,128)(2,1)S(1)}, bf16[512,640]{1,0:T(8,128)(2,1)S(1)}, u32[]{:S(2)}, u32[]{:S(2)}) %collective-permute-start.44) | collective-permute-done | bytes 655392 | tf_op jit(solution)/shard_map/ppermute | solution.py:599
  114.2 3.7 %collective-permute-start.35 = (bf16[512,768]{1,0:T(8,128)(2,1)S(1)}, bf16[512,768]{1,0:T(8,128)(2,1)S(1)}, u32[]{:S(2)}, u32[]{:S(2)}) collective-permute-start(bf16[512,768]{1,0:T(8,128)(2,1)S(1)} %get-tuple-element.119), channel_id=1, source_target_pairs={{0,96},{32,64},{64,32},{96,0},{1,97},{33,65},{65,33},{97,1},{2,98}... | collective-permute-start | bytes 2359304 | tf_op jit(solution)/shard_map/ppermute | solution.py:598
  118.1 6.2 %collective-permute-done.40.refs_1_ = bf16[512,768]{1,0:T(8,128)(2,1)S(1)} collective-permute-done((bf16[512,768]{1,0:T(8,128)(2,1)S(1)}, bf16[512,768]{1,0:T(8,128)(2,1)S(1)}, u32[]{:S(2)}, u32[]{:S(2)}) %collective-permute-start.40) | collective-permute-done | bytes 786464 | tf_op jit(solution)/shard_map/ppermute | solution.py:598
  124.3 3.7 %collective-permute-start.31 = (bf16[512,896]{1,0:T(8,128)(2,1)S(1)}, bf16[512,896]{1,0:T(8,128)(2,1)S(1)}, u32[]{:S(2)}, u32[]{:S(2)}) collective-permute-start(bf16[512,896]{1,0:T(8,128)(2,1)S(1)} %half_add.9), channel_id=1, source_target_pairs={{0,96},{32,64},{64,32},{96,0},{1,97},{33,65},{65,33},{97,1},{2,98}... | collective-permute-start | bytes 2752520 | tf_op jit(solution)/shard_map/ppermute | solution.py:601
  128.0 11.2 %collective-permute-done.39.refs_1_ = bf16[512,768]{1,0:T(8,128)(2,1)S(1)} collective-permute-done((bf16[512,768]{1,0:T(8,128)(2,1)S(1)}, bf16[512,768]{1,0:T(8,128)(2,1)S(1)}, u32[]{:S(2)}, u32[]{:S(2)}) %collective-permute-start.39) | collective-permute-done | bytes 786464 | tf_op jit(solution)/shard_map/ppermute | solution.py:599
  139.1 3.7 %collective-permute-start.34 = (bf16[512,768]{1,0:T(8,128)(2,1)S(1)}, bf16[512,768]{1,0:T(8,128)(2,1)S(1)}, u32[]{:S(2)}, u32[]{:S(2)}) collective-permute-start(bf16[512,768]{1,0:T(8,128)(2,1)S(1)} %get-tuple-element.118), channel_id=1, source_target_pairs={{0,96},{32,64},{64,32},{96,0},{1,97},{33,65},{65,33},{97,1},{2,98}... | collective-permute-start | bytes 2359304 | tf_op jit(solution)/shard_map/ppermute | solution.py:599
  144.5 11.4 %collective-permute-done.31.refs_1_ = bf16[512,896]{1,0:T(8,128)(2,1)S(1)} collective-permute-done((bf16[512,896]{1,0:T(8,128)(2,1)S(1)}, bf16[512,896]{1,0:T(8,128)(2,1)S(1)}, u32[]{:S(2)}, u32[]{:S(2)}) %collective-permute-start.31) | collective-permute-done | bytes 917536 | tf_op jit(solution)/shard_map/ppermute | solution.py:601
  157.6 14.0 %collective-permute-done.34.refs_1_ = bf16[512,768]{1,0:T(8,128)(2,1)S(1)} collective-permute-done((bf16[512,768]{1,0:T(8,128)(2,1)S(1)}, bf16[512,768]{1,0:T(8,128)(2,1)S(1)}, u32[]{:S(2)}, u32[]{:S(2)}) %collective-permute-start.34) | collective-permute-done | bytes 786464 | tf_op jit(solution)/shard_map/ppermute | solution.py:599
  171.7 2.7 %collective-permute-start.23 = (bf16[512,384]{1,0:T(8,128)(2,1)S(1)}, bf16[512,384]{1,0:T(8,128)(2,1)S(1)}, u32[]{:S(2)}, u32[]{:S(2)}) collective-permute-start(bf16[512,384]{1,0:T(8,128)(2,1)S(1)} %get-tuple-element.101), channel_id=1, source_target_pairs={{0,4},{2,6},{4,0},{6,2},{1,5},{3,7},{5,1},{7,3},{8,12},{10,14},{12... | collective-permute-start | bytes 1179656 | tf_op jit(solution)/shard_map/ppermute | solution.py:481
  176.1 7.0 %collective-permute-done.32.refs_1_ = bf16[256,896]{1,0:T(8,128)(2,1)S(1)} collective-permute-done((bf16[256,896]{1,0:T(8,128)(2,1)S(1)}, bf16[256,896]{1,0:T(8,128)(2,1)S(1)}, u32[]{:S(2)}, u32[]{:S(2)}) %collective-permute-start.32) | collective-permute-done | bytes 458784 | tf_op jit(solution)/shard_map/ppermute | solution.py:605
  183.1 2.7 %collective-permute-start.47 = (bf16[256,640]{1,0:T(8,128)(2,1)S(1)}, bf16[256,640]{1,0:T(8,128)(2,1)S(1)}, u32[]{:S(2)}, u32[]{:S(2)}) collective-permute-start(bf16[256,640]{1,0:T(8,128)(2,1)S(1)} %get-tuple-element.135), channel_id=1, source_target_pairs={{0,96},{32,64},{64,32},{96,0},{1,97},{33,65},{65,33},{97,1},{2,98}... | collective-permute-start | bytes 983048 | tf_op jit(solution)/shard_map/ppermute | solution.py:605
  185.8 5.5 %collective-permute-done.22.refs_1_ = bf16[512,384]{1,0:T(8,128)(2,1)S(1)} collective-permute-done((bf16[512,384]{1,0:T(8,128)(2,1)S(1)}, bf16[512,384]{1,0:T(8,128)(2,1)S(1)}, u32[]{:S(2)}, u32[]{:S(2)}) %collective-permute-start.22) | collective-permute-done | bytes 393248 | tf_op jit(solution)/shard_map/ppermute | solution.py:481
  192.9 2.8 %collective-permute-start.43 = (bf16[128,768]{1,0:T(8,128)(2,1)S(1)}, bf16[128,768]{1,0:T(8,128)(2,1)S(1)}, u32[]{:S(2)}, u32[]{:S(2)}) collective-permute-start(bf16[128,768]{1,0:T(8,128)(2,1)S(1)} %get-tuple-element.130), channel_id=1, source_target_pairs={{0,96},{32,64},{64,32},{96,0},{1,97},{33,65},{65,33},{97,1},{2,98}... | collective-permute-start | bytes 589832 | tf_op jit(solution)/shard_map/ppermute | solution.py:605
  199.6 4.5 %collective-permute-done.25.right = f32[48,256]{1,0:T(8,128)S(1)} collective-permute-done((f32[48,256]{1,0:T(8,128)S(1)}, f32[48,256]{1,0:T(8,128)S(1)}, u32[]{:S(2)}, u32[]{:S(2)}) %collective-permute-start.25) | collective-permute-done | bytes 49184 | tf_op jit(solution)/shard_map/ppermute | solution.py:99
  204.9 3.3 %collective-permute-done.26.right = f32[48,256]{1,0:T(8,128)S(1)} collective-permute-done((f32[48,256]{1,0:T(8,128)S(1)}, f32[48,256]{1,0:T(8,128)S(1)}, u32[]{:S(2)}, u32[]{:S(2)}) %collective-permute-start.26) | collective-permute-done | bytes 49184 | tf_op jit(solution)/shard_map/ppermute | solution.py:99
  208.2 2.7 %collective-permute-start.27 = (f32[48,256]{1,0:T(8,128)S(1)}, f32[48,256]{1,0:T(8,128)S(1)}, u32[]{:S(2)}, u32[]{:S(2)}) collective-permute-start(f32[48,256]{1,0:T(8,128)S(1)} %pair_added.5.mine), channel_id=1, source_target_pairs={{0,24},{8,16},{16,8},{24,0},{1,25},{9,17},{17,9},{25,1},{2,26},{10... | collective-permute-start | bytes 147464 | tf_op jit(solution)/shard_map/ppermute | solution.py:99
  (109 shorter events, 46.5 us)
Async XLA Ops:
  1.9 20.6 %collective-permute-start.6 = (bf16[768,256]{1,0:T(8,128)(2,1)S(1)}, bf16[768,256]{1,0:T(8,128)(2,1)S(1)}, u32[]{:S(2)}, u32[]{:S(2)}) collective-permute-start(bf16[768,256]{1,0:T(8,128)(2,1)S(1)} %get-tuple-element.76.refs_0_), channel_id=1, source_target_pairs={{0,6},{2,0},{4,2},{6,4},{1,7},{3,1},{5,3},{7,5},{8,14},{10,8},{12,... | collective-permute-start | bytes 1179656 | tf_op jit(solution)/shard_map/ppermute | solution.py:66
  2.7 19.8 %collective-permute-start.7 = (bf16[768,256]{1,0:T(8,128)(2,1)S(1)}, bf16[768,256]{1,0:T(8,128)(2,1)S(1)}, u32[]{:S(2)}, u32[]{:S(2)}) collective-permute-start(bf16[768,256]{1,0:T(8,128)(2,1)S(1)} %get-tuple-element.76.refs_0_), channel_id=1, source_target_pairs={{0,4},{2,6},{4,0},{6,2},{1,5},{3,7},{5,1},{7,3},{8,12},{10,14},{12... | collective-permute-start | bytes 1179656 | tf_op jit(solution)/shard_map/ppermute | solution.py:66
  3.5 23.3 %collective-permute-start.8 = (bf16[768,256]{1,0:T(8,128)(2,1)S(1)}, bf16[768,256]{1,0:T(8,128)(2,1)S(1)}, u32[]{:S(2)}, u32[]{:S(2)}) collective-permute-start(bf16[768,256]{1,0:T(8,128)(2,1)S(1)} %get-tuple-element.76.refs_0_), channel_id=1, source_target_pairs={{0,2},{2,4},{4,6},{6,0},{1,3},{3,5},{5,7},{7,1},{8,10},{10,12},{12... | collective-permute-start | bytes 1179656 | tf_op jit(solution)/shard_map/ppermute | solution.py:66
  7.7 15.2 %collective-permute-start.1 = (f32[48,256]{1,0:T(8,128)S(1)}, f32[48,256]{1,0:T(8,128)S(1)}, u32[]{:S(2)}, u32[]{:S(2)}) collective-permute-start(f32[48,256]{1,0:T(8,128)S(1)} %get-tuple-element.74.refs_0_), channel_id=1, source_target_pairs={{0,96},{32,0},{64,32},{96,64},{1,97},{33,1},{65,33},{97,65},{2,98}... | collective-permute-start | bytes 147464 | tf_op jit(solution)/shard_map/ppermute | solution.py:113
  11.9 47.1 %collective-permute-start.9 = (bf16[768,256]{1,0:T(8,128)(2,1)S(1)}, bf16[768,256]{1,0:T(8,128)(2,1)S(1)}, u32[]{:S(2)}, u32[]{:S(2)}) collective-permute-start(bf16[768,256]{1,0:T(8,128)(2,1)S(1)} %get-tuple-element.76.refs_0_), channel_id=1, source_target_pairs={{0,1},{1,0},{2,3},{3,2},{4,5},{5,4},{6,7},{7,6},{8,9},{9,8},{10,11... | collective-permute-start | bytes 1179656 | tf_op jit(solution)/shard_map/ppermute | solution.py:70
  22.4 37.1 %collective-permute-start.10 = (bf16[768,256]{1,0:T(8,128)(2,1)S(1)}, bf16[768,256]{1,0:T(8,128)(2,1)S(1)}, u32[]{:S(2)}, u32[]{:S(2)}) collective-permute-start(bf16[768,256]{1,0:T(8,128)(2,1)S(1)} %collective-permute-done.6.refs_1_), channel_id=1, source_target_pairs={{0,1},{1,0},{2,3},{3,2},{4,5},{5,4},{6,7},{7,6},{8,9},{9,8},{10,11... | collective-permute-start | bytes 1179656 | tf_op jit(solution)/shard_map/ppermute | solution.py:70
  22.5 37.2 %collective-permute-start.11 = (bf16[768,256]{1,0:T(8,128)(2,1)S(1)}, bf16[768,256]{1,0:T(8,128)(2,1)S(1)}, u32[]{:S(2)}, u32[]{:S(2)}) collective-permute-start(bf16[768,256]{1,0:T(8,128)(2,1)S(1)} %collective-permute-done.7.refs_2_), channel_id=1, source_target_pairs={{0,1},{1,0},{2,3},{3,2},{4,5},{5,4},{6,7},{7,6},{8,9},{9,8},{10,11... | collective-permute-start | bytes 1179656 | tf_op jit(solution)/shard_map/ppermute | solution.py:70
  26.8 39.0 %collective-permute-start.12 = (bf16[768,256]{1,0:T(8,128)(2,1)S(1)}, bf16[768,256]{1,0:T(8,128)(2,1)S(1)}, u32[]{:S(2)}, u32[]{:S(2)}) collective-permute-start(bf16[768,256]{1,0:T(8,128)(2,1)S(1)} %collective-permute-done.8.refs_3_), channel_id=1, source_target_pairs={{0,1},{1,0},{2,3},{3,2},{4,5},{5,4},{6,7},{7,6},{8,9},{9,8},{10,11... | collective-permute-start | bytes 1179656 | tf_op jit(solution)/shard_map/ppermute | solution.py:70
  72.2 31.7 %collective-permute-start.45 = (bf16[512,640]{1,0:T(8,128)(2,1)S(1)}, bf16[512,640]{1,0:T(8,128)(2,1)S(1)}, u32[]{:S(2)}, u32[]{:S(2)}) collective-permute-start(bf16[512,640]{1,0:T(8,128)(2,1)S(1)} %get-tuple-element.133), channel_id=1, source_target_pairs={{0,24},{8,16},{16,8},{24,0},{1,25},{9,17},{17,9},{25,1},{2,26},{10... | collective-permute-start | bytes 1966088 | tf_op jit(solution)/shard_map/ppermute | solution.py:598
  78.9 38.9 %collective-permute-start.30 = (bf16[512,768]{1,0:T(8,128)(2,1)S(1)}, bf16[512,768]{1,0:T(8,128)(2,1)S(1)}, u32[]{:S(2)}, u32[]{:S(2)}) collective-permute-start(bf16[512,768]{1,0:T(8,128)(2,1)S(1)} %get-tuple-element.112), channel_id=1, source_target_pairs={{0,32},{32,0},{64,96},{96,64},{1,33},{33,1},{65,97},{97,65},{2,34}... | collective-permute-start | bytes 2359304 | tf_op jit(solution)/shard_map/ppermute | solution.py:598
  80.6 23.3 %collective-permute-start.29 = (bf16[1024,128]{1,0:T(8,128)(2,1)S(1)}, bf16[1024,128]{1,0:T(8,128)(2,1)S(1)}, u32[]{:S(2)}, u32[]{:S(2)}) collective-permute-start(bf16[1024,128]{1,0:T(8,128)(2,1)S(1)} %get-tuple-element.111), channel_id=1, source_target_pairs={{0,32},{32,0},{64,96},{96,64},{1,33},{33,1},{65,97},{97,65},{2,34}... | collective-permute-start | bytes 786440 | tf_op jit(solution)/shard_map/ppermute | solution.py:597
  95.7 48.3 %collective-permute-start.20 = (bf16[8,256,384]{2,1,0:T(8,128)(2,1)S(1)}, bf16[8,256,384]{2,1,0:T(8,128)(2,1)S(1)}, u32[]{:S(2)}, u32[]{:S(2)}) collective-permute-start(bf16[8,256,384]{2,1,0:T(8,128)(2,1)S(1)} %get-tuple-element.97), channel_id=1, source_target_pairs={{0,1},{1,0},{2,3},{3,2},{4,5},{5,4},{6,7},{7,6},{8,9},{9,8},{10,11... | collective-permute-start | bytes 4718600 | tf_op jit(solution)/shard_map/ppermute | solution.py:468
  95.8 18.3 %collective-permute-start.44 = (bf16[512,640]{1,0:T(8,128)(2,1)S(1)}, bf16[512,640]{1,0:T(8,128)(2,1)S(1)}, u32[]{:S(2)}, u32[]{:S(2)}) collective-permute-start(bf16[512,640]{1,0:T(8,128)(2,1)S(1)} %get-tuple-element.132), channel_id=1, source_target_pairs={{0,24},{8,16},{16,8},{24,0},{1,25},{9,17},{17,9},{25,1},{2,26},{10... | collective-permute-start | bytes 1966088 | tf_op jit(solution)/shard_map/ppermute | solution.py:599
  103.9 20.4 %collective-permute-start.40 = (bf16[512,768]{1,0:T(8,128)(2,1)S(1)}, bf16[512,768]{1,0:T(8,128)(2,1)S(1)}, u32[]{:S(2)}, u32[]{:S(2)}) collective-permute-start(bf16[512,768]{1,0:T(8,128)(2,1)S(1)} %get-tuple-element.126), channel_id=1, source_target_pairs={{0,8},{8,0},{16,24},{24,16},{1,9},{9,1},{17,25},{25,17},{2,10},{10... | collective-permute-start | bytes 2359304 | tf_op jit(solution)/shard_map/ppermute | solution.py:598
  103.9 35.2 %collective-permute-start.39 = (bf16[512,768]{1,0:T(8,128)(2,1)S(1)}, bf16[512,768]{1,0:T(8,128)(2,1)S(1)}, u32[]{:S(2)}, u32[]{:S(2)}) collective-permute-start(bf16[512,768]{1,0:T(8,128)(2,1)S(1)} %get-tuple-element.125), channel_id=1, source_target_pairs={{0,8},{8,0},{16,24},{24,16},{1,9},{9,1},{17,25},{25,17},{2,10},{10... | collective-permute-start | bytes 2359304 | tf_op jit(solution)/shard_map/ppermute | solution.py:599
  114.2 28.8 %collective-permute-start.35 = (bf16[512,768]{1,0:T(8,128)(2,1)S(1)}, bf16[512,768]{1,0:T(8,128)(2,1)S(1)}, u32[]{:S(2)}, u32[]{:S(2)}) collective-permute-start(bf16[512,768]{1,0:T(8,128)(2,1)S(1)} %get-tuple-element.119), channel_id=1, source_target_pairs={{0,96},{32,64},{64,32},{96,0},{1,97},{33,65},{65,33},{97,1},{2,98}... | collective-permute-start | bytes 2359304 | tf_op jit(solution)/shard_map/ppermute | solution.py:598
  117.9 25.9 %collective-permute-start.28 = (bf16[512,768]{1,0:T(8,128)(2,1)S(1)}, bf16[512,768]{1,0:T(8,128)(2,1)S(1)}, u32[]{:S(2)}, u32[]{:S(2)}) collective-permute-start(bf16[512,768]{1,0:T(8,128)(2,1)S(1)} %get-tuple-element.109), channel_id=1, source_target_pairs={{0,32},{32,0},{64,96},{96,64},{1,33},{33,1},{65,97},{97,65},{2,34}... | collective-permute-start | bytes 2359304 | tf_op jit(solution)/shard_map/ppermute | solution.py:599
  124.3 31.6 %collective-permute-start.31 = (bf16[512,896]{1,0:T(8,128)(2,1)S(1)}, bf16[512,896]{1,0:T(8,128)(2,1)S(1)}, u32[]{:S(2)}, u32[]{:S(2)}) collective-permute-start(bf16[512,896]{1,0:T(8,128)(2,1)S(1)} %half_add.9), channel_id=1, source_target_pairs={{0,96},{32,64},{64,32},{96,0},{1,97},{33,65},{65,33},{97,1},{2,98}... | collective-permute-start | bytes 2752520 | tf_op jit(solution)/shard_map/ppermute | solution.py:601
  139.1 32.5 %collective-permute-start.34 = (bf16[512,768]{1,0:T(8,128)(2,1)S(1)}, bf16[512,768]{1,0:T(8,128)(2,1)S(1)}, u32[]{:S(2)}, u32[]{:S(2)}) collective-permute-start(bf16[512,768]{1,0:T(8,128)(2,1)S(1)} %get-tuple-element.118), channel_id=1, source_target_pairs={{0,96},{32,64},{64,32},{96,0},{1,97},{33,65},{65,33},{97,1},{2,98}... | collective-permute-start | bytes 2359304 | tf_op jit(solution)/shard_map/ppermute | solution.py:599
  143.0 28.7 %collective-permute-start.41 = (bf16[512,768]{1,0:T(8,128)(2,1)S(1)}, bf16[512,768]{1,0:T(8,128)(2,1)S(1)}, u32[]{:S(2)}, u32[]{:S(2)}) collective-permute-start(bf16[512,768]{1,0:T(8,128)(2,1)S(1)} %half_add.13), channel_id=1, source_target_pairs={{0,24},{8,16},{16,8},{24,0},{1,25},{9,17},{17,9},{25,1},{2,26},{10... | collective-permute-start | bytes 2359304 | tf_op jit(solution)/shard_map/ppermute | solution.py:601
  143.8 30.9 %collective-permute-start.36 = (bf16[512,768]{1,0:T(8,128)(2,1)S(1)}, bf16[512,768]{1,0:T(8,128)(2,1)S(1)}, u32[]{:S(2)}, u32[]{:S(2)}) collective-permute-start(bf16[512,768]{1,0:T(8,128)(2,1)S(1)} %half_add.11), channel_id=1, source_target_pairs={{0,32},{32,0},{64,96},{96,64},{1,33},{33,1},{65,97},{97,65},{2,34}... | collective-permute-start | bytes 2359304 | tf_op jit(solution)/shard_map/ppermute | solution.py:601
  144.0 27.6 %collective-permute-start.46 = (bf16[512,640]{1,0:T(8,128)(2,1)S(1)}, bf16[512,640]{1,0:T(8,128)(2,1)S(1)}, u32[]{:S(2)}, u32[]{:S(2)}) collective-permute-start(bf16[512,640]{1,0:T(8,128)(2,1)S(1)} %half_add.15), channel_id=1, source_target_pairs={{0,8},{8,0},{16,24},{24,16},{1,9},{9,1},{17,25},{25,17},{2,10},{10... | collective-permute-start | bytes 1966088 | tf_op jit(solution)/shard_map/ppermute | solution.py:601
  155.9 19.3 %collective-permute-start.21 = (bf16[512,384]{1,0:T(8,128)(2,1)S(1)}, bf16[512,384]{1,0:T(8,128)(2,1)S(1)}, u32[]{:S(2)}, u32[]{:S(2)}) collective-permute-start(bf16[512,384]{1,0:T(8,128)(2,1)S(1)} %get-tuple-element.99), channel_id=1, source_target_pairs={{0,2},{2,4},{4,6},{6,0},{1,3},{3,5},{5,7},{7,1},{8,10},{10,12},{12... | collective-permute-start | bytes 1179656 | tf_op jit(solution)/shard_map/ppermute | solution.py:481
  171.6 19.6 %collective-permute-start.22 = (bf16[512,384]{1,0:T(8,128)(2,1)S(1)}, bf16[512,384]{1,0:T(8,128)(2,1)S(1)}, u32[]{:S(2)}, u32[]{:S(2)}) collective-permute-start(bf16[512,384]{1,0:T(8,128)(2,1)S(1)} %get-tuple-element.100), channel_id=1, source_target_pairs={{0,6},{2,0},{4,2},{6,4},{1,7},{3,1},{5,3},{7,5},{8,14},{10,8},{12,... | collective-permute-start | bytes 1179656 | tf_op jit(solution)/shard_map/ppermute | solution.py:481
  171.7 20.1 %collective-permute-start.23 = (bf16[512,384]{1,0:T(8,128)(2,1)S(1)}, bf16[512,384]{1,0:T(8,128)(2,1)S(1)}, u32[]{:S(2)}, u32[]{:S(2)}) collective-permute-start(bf16[512,384]{1,0:T(8,128)(2,1)S(1)} %get-tuple-element.101), channel_id=1, source_target_pairs={{0,4},{2,6},{4,0},{6,2},{1,5},{3,7},{5,1},{7,3},{8,12},{10,14},{12... | collective-permute-start | bytes 1179656 | tf_op jit(solution)/shard_map/ppermute | solution.py:481
  174.7 18.0 %collective-permute-start.42 = (bf16[256,768]{1,0:T(8,128)(2,1)S(1)}, bf16[256,768]{1,0:T(8,128)(2,1)S(1)}, u32[]{:S(2)}, u32[]{:S(2)}) collective-permute-start(bf16[256,768]{1,0:T(8,128)(2,1)S(1)} %get-tuple-element.128), channel_id=1, source_target_pairs={{0,32},{32,0},{64,96},{96,64},{1,33},{33,1},{65,97},{97,65},{2,34}... | collective-permute-start | bytes 1179656 | tf_op jit(solution)/shard_map/ppermute | solution.py:605
  175.2 20.4 %collective-permute-start.37 = (bf16[256,768]{1,0:T(8,128)(2,1)S(1)}, bf16[256,768]{1,0:T(8,128)(2,1)S(1)}, u32[]{:S(2)}, u32[]{:S(2)}) collective-permute-start(bf16[256,768]{1,0:T(8,128)(2,1)S(1)} %get-tuple-element.121), channel_id=1, source_target_pairs={{0,24},{8,16},{16,8},{24,0},{1,25},{9,17},{17,9},{25,1},{2,26},{10... | collective-permute-start | bytes 1179656 | tf_op jit(solution)/shard_map/ppermute | solution.py:605
  183.1 14.0 %collective-permute-start.47 = (bf16[256,640]{1,0:T(8,128)(2,1)S(1)}, bf16[256,640]{1,0:T(8,128)(2,1)S(1)}, u32[]{:S(2)}, u32[]{:S(2)}) collective-permute-start(bf16[256,640]{1,0:T(8,128)(2,1)S(1)} %get-tuple-element.135), channel_id=1, source_target_pairs={{0,96},{32,64},{64,32},{96,0},{1,97},{33,65},{65,33},{97,1},{2,98}... | collective-permute-start | bytes 983048 | tf_op jit(solution)/shard_map/ppermute | solution.py:605
  191.3 23.8 %collective-permute-start.33 = (bf16[128,896]{1,0:T(8,128)(2,1)S(1)}, bf16[128,896]{1,0:T(8,128)(2,1)S(1)}, u32[]{:S(2)}, u32[]{:S(2)}) collective-permute-start(bf16[128,896]{1,0:T(8,128)(2,1)S(1)} %get-tuple-element.116), channel_id=1, source_target_pairs={{0,24},{8,16},{16,8},{24,0},{1,25},{9,17},{17,9},{25,1},{2,26},{10... | collective-permute-start | bytes 688136 | tf_op jit(solution)/shard_map/ppermute | solution.py:605
  192.9 22.2 %collective-permute-start.43 = (bf16[128,768]{1,0:T(8,128)(2,1)S(1)}, bf16[128,768]{1,0:T(8,128)(2,1)S(1)}, u32[]{:S(2)}, u32[]{:S(2)}) collective-permute-start(bf16[128,768]{1,0:T(8,128)(2,1)S(1)} %get-tuple-element.130), channel_id=1, source_target_pairs={{0,96},{32,64},{64,32},{96,0},{1,97},{33,65},{65,33},{97,1},{2,98}... | collective-permute-start | bytes 589832 | tf_op jit(solution)/shard_map/ppermute | solution.py:605
  195.7 19.4 %collective-permute-start.38 = (bf16[128,768]{1,0:T(8,128)(2,1)S(1)}, bf16[128,768]{1,0:T(8,128)(2,1)S(1)}, u32[]{:S(2)}, u32[]{:S(2)}) collective-permute-start(bf16[128,768]{1,0:T(8,128)(2,1)S(1)} %get-tuple-element.123), channel_id=1, source_target_pairs={{0,8},{8,0},{16,24},{24,16},{1,9},{9,1},{17,25},{25,17},{2,10},{10... | collective-permute-start | bytes 589832 | tf_op jit(solution)/shard_map/ppermute | solution.py:605
  197.2 17.9 %collective-permute-start.48 = (bf16[128,640]{1,0:T(8,128)(2,1)S(1)}, bf16[128,640]{1,0:T(8,128)(2,1)S(1)}, u32[]{:S(2)}, u32[]{:S(2)}) collective-permute-start(bf16[128,640]{1,0:T(8,128)(2,1)S(1)} %get-tuple-element.137), channel_id=1, source_target_pairs={{0,32},{32,0},{64,96},{96,64},{1,33},{33,1},{65,97},{97,65},{2,34}... | collective-permute-start | bytes 491528 | tf_op jit(solution)/shard_map/ppermute | solution.py:605
  (20 other events, 138.1 us)
